TPU v7x, 128 devices: a whole 4x4x4 slice. The times are simulated.
128 devices in a mesh: row: 8 (over x, core), col: 16 (over y, z).
Axes of the slice: x: 4, y: 4, z: 4, core: 2. Of those that a mesh axis runs over, the one named last changes fastest.
Arguments:
- velocity: float32 [3, 2, 128, 512, 256], P(None, None, 'row', 'col'), may hold values from -6 to 6
- register: float32 [3, 2, 128, 512, 256], P(None, None, 'row', 'col'), may hold values from -6 to 6
- offsets: int32 [256], replicated, may hold values from -2 to 2, as said below
- remesh_flag: int32 [256], replicated, may hold values from 0 to 1, as said below
- keep_blocks: int32 [16], replicated, may hold values 0 or 1
Outputs:
- velocity_next: float32 [3, 2, 128, 512, 256], P(None, None, 'row', 'col')
Inputs may be any that keep to these rules, and one draw needn't show every extreme that they name: offsets[j] is 0 or has the sign of ky = j - 128. On each side of ky = 0 the planes of magnitude 1 form one run of consecutive ky, and the planes of magnitude 2 the run that follows it directly, farther from ky = 0. Each of -2, -1, 1 and 2 is carried by half of 32 to 32 planes. Each nonzero value of offsets[j] remesh_flag[j] is taken by at most 32 planes, and in every draw one of them by exactly 32 planes.
All inputs are finite; a program needn't handle non-finite values.
Results may differ from a plain program's by a relative error of at most 0.0055.
Values may be sent and summed in bfloat16 or wider, within the bound.
A program may use at most 192 MiB of HBM per device.

v0:
```python
import math

import jax
import jax.numpy as jnp
from jax import lax
from jax.sharding import PartitionSpec as P

NX = 512
NY = 256
NZ = 256
NZH = 128
MX = 768
MY = 384
MZ = 384
SHIFT_CAP = 32


SHEAR_RATE = 40.0
SHEAR_TIME = 0.3
VISCOSITY = 0.0015
TIME_STEP = 0.008
REGISTER_WEIGHT = -153.0 / 128.0
UPDATE_WEIGHT = 8.0 / 15.0
PRODUCT_PAIRS = ((0, 0), (0, 1), (0, 2), (1, 1), (1, 2), (2, 2))
PAIR_LOOKUP = ((0, 1, 2), (1, 3, 4), (2, 4, 5))
OFFSET_VALUES = (-2, -1, 1, 2)


def items_in_groups(array, axis, split_dim, concat_dim, work, item_dim, out_dim):
    items = jax.tree.leaves(array)[0].shape[item_dim]
    count = 2 if items % 2 == 0 else 1
    done = []
    for k in range(count):
        group = jax.tree.map(
            lambda a: lax.slice_in_dim(
                a, k * (items // count), (k + 1) * (items // count), axis=item_dim
            ),
            array,
        )
        done.append(
            work(
                lax.all_to_all(
                    group, axis, split_axis=split_dim, concat_axis=concat_dim, tiled=True
                )
            )
        )
    return jax.tree.map(lambda *parts: jnp.concatenate(parts, axis=out_dim), *done)


def from_behind(block, axis, distance):
    devices = range(lax.axis_size(axis))
    route = [(i - distance, i) for i in devices if i - distance in devices]
    return lax.ppermute(block, axis, route)


def phase_angles(contracted, produced, period):
    phase_turns = jnp.mod(contracted[:, None] * produced[None, :], period)
    return phase_turns.astype(jnp.float32) * (2.0 * math.pi / period)


def complex_table(contracted, produced, period, direction):
    angles = phase_angles(contracted, produced, period)
    cosine = jnp.cos(angles)
    sine_part = direction * jnp.sin(angles)
    upper_rows = jnp.stack([cosine, sine_part], axis=1)
    lower_rows = jnp.stack([-sine_part, cosine], axis=1)
    return jnp.stack([upper_rows, lower_rows], axis=0).astype(jnp.bfloat16)


def inverse_real_table(mode_list, points, period):
    angles = phase_angles(mode_list, points, period)
    weights = jnp.where(mode_list == 0, 1.0, 2.0).astype(jnp.float32)[:, None]
    return jnp.stack([weights * jnp.cos(angles), -weights * jnp.sin(angles)], axis=0).astype(
        jnp.bfloat16
    )


def forward_real_table(points, mode_list, period):
    angles = phase_angles(points, mode_list, period)
    return jnp.stack([jnp.cos(angles), -jnp.sin(angles)], axis=1).astype(jnp.bfloat16)


def tendency_update(spectra, velocity, register, kx_values, ky_values, kz_values):
    wave_x = kx_values[None, :, None] - SHEAR_TIME * ky_values[None, None, :]
    wave_y = ky_values[None, None, :]
    wave_z = kz_values[:, None, None]
    wave_list = (wave_x, wave_y, wave_z)
    squared = wave_x * wave_x + wave_y * wave_y + wave_z * wave_z
    inverse = 1.0 / jnp.maximum(squared, 1.0)
    advect_real = [
        sum((wave_list[source] * spectra[PAIR_LOOKUP[target][source], 1] for source in range(3)))
        for target in range(3)
    ]
    advect_imag = [
        -sum((wave_list[source] * spectra[PAIR_LOOKUP[target][source], 0] for source in range(3)))
        for target in range(3)
    ]
    diverge_real = sum((wave_list[target] * advect_real[target] for target in range(3)))
    diverge_imag = sum((wave_list[target] * advect_imag[target] for target in range(3)))
    pressure_lift = 2.0 * SHEAR_RATE * wave_y * inverse
    results = []
    for target in range(3):
        halves = []
        for half_index, advect, diverge in (
            (0, advect_real, diverge_real),
            (1, advect_imag, diverge_imag),
        ):
            rate_value = advect[target] - wave_list[target] * diverge * inverse
            rate_value = rate_value + wave_list[target] * pressure_lift * velocity[0, half_index]
            rate_value = rate_value - VISCOSITY * squared * velocity[target, half_index]
            if target == 1:
                rate_value = rate_value - SHEAR_RATE * velocity[0, half_index]
            increment = REGISTER_WEIGHT * register[target, half_index] + TIME_STEP * rate_value
            halves.append(velocity[target, half_index] + UPDATE_WEIGHT * increment)
        results.append(jnp.stack(halves))
    return jnp.stack(results)


def local(velocity, register, offsets, remesh_flag, keep_blocks):
    rows_count = lax.axis_size("row")
    cols_count = lax.axis_size("col")
    row_index = lax.axis_index("row")
    col_index = lax.axis_index("col")
    slab_kz = velocity.shape[2]
    slab_kx = velocity.shape[3]
    y_cols = MY // cols_count
    y_both = y_cols // rows_count
    inverse_scale = 1.0 / math.sqrt(NX * NY * NZ)
    forward_scale = math.sqrt(NX * NY * NZ) / (MX * MY * MZ)
    y_order = jnp.arange(MY, dtype=jnp.int32)
    owner_col = y_order // y_cols
    within_col = y_order % y_cols
    y_permuted = (within_col // y_both * cols_count + owner_col) * y_both + within_col % y_both
    x_points = jnp.arange(MX, dtype=jnp.int32)
    z_points = jnp.arange(MZ, dtype=jnp.int32)
    kx_all = jnp.arange(NX, dtype=jnp.int32) - NX // 2
    ky_all = jnp.arange(NY, dtype=jnp.int32) - NY // 2
    kz_all = jnp.arange(NZH, dtype=jnp.int32)
    kx_local = col_index * slab_kx + jnp.arange(slab_kx, dtype=jnp.int32) - NX // 2
    kz_local = row_index * slab_kz + jnp.arange(slab_kz, dtype=jnp.int32)
    y_inverse = complex_table(ky_all, y_permuted, MY, 1.0)
    x_inverse = complex_table(kx_all, x_points, MX, 1.0)
    z_inverse = inverse_real_table(kz_all, z_points, MZ)
    z_forward = forward_real_table(z_points, kz_all, MZ)
    x_forward = complex_table(x_points, kx_all, MX, -1.0)
    spectral = velocity.astype(jnp.bfloat16)
    along_y = jnp.einsum(
        "crlij,rjsq->csliq", spectral, y_inverse, preferred_element_type=jnp.float32
    ).astype(jnp.bfloat16)

    def inverse_x(items):
        return jnp.einsum(
            "crliq,risp->cslqp", items, x_inverse, preferred_element_type=jnp.float32
        ).astype(jnp.bfloat16)

    along_x = items_in_groups(along_y, "col", 4, 3, inverse_x, 2, 2)
    fields = (
        jnp.einsum(
            "crlab,rlz->cabz",
            lax.all_to_all(along_x, "row", split_axis=3, concat_axis=2, tiled=True),
            z_inverse,
            preferred_element_type=jnp.float32,
        )
        * inverse_scale
    )
    products = jnp.stack(
        [fields[left_factor] * fields[right_factor] for left_factor, right_factor in PRODUCT_PAIRS]
    ).astype(jnp.bfloat16)
    modes_z = (
        jnp.einsum("eabz,zsl->esabl", products, z_forward, preferred_element_type=jnp.float32)
        .astype(jnp.bfloat16)
        .reshape(6, 2, y_both, MX, rows_count, slab_kz)
    )
    x_split = x_forward.reshape(2, MX, 2, cols_count, slab_kx)
    arranged = jnp.einsum(
        "eryxab,rxscd->esyacbd", modes_z, x_split, preferred_element_type=jnp.float32
    ).astype(jnp.bfloat16)
    arranged = arranged.reshape(6, 2, y_both, rows_count * cols_count, slab_kz * slab_kx)
    gathered = lax.all_to_all(arranged, ("row", "col"), split_axis=3, concat_axis=2, tiled=True)
    gathered = gathered.reshape(6, 2, MY, slab_kz, slab_kx)
    y_forward = complex_table(y_order, ky_all, MY, -1.0)
    spectra = jnp.einsum(
        "erqli,rqsj->eslij", gathered, y_forward, preferred_element_type=jnp.float32
    )
    spectra = spectra * forward_scale
    updated = tendency_update(
        spectra,
        velocity,
        register,
        kx_local.astype(jnp.float32),
        ky_all.astype(jnp.float32),
        kz_local.astype(jnp.float32),
    )
    moved_by = offsets * remesh_flag
    remeshed = updated * (moved_by == 0).astype(jnp.float32)
    slot_ids = jnp.arange(SHIFT_CAP, dtype=jnp.int32)
    columns = []
    for shift_by in OFFSET_VALUES:
        marked = moved_by == shift_by
        ranked = jnp.cumsum(marked.astype(jnp.int32)) - 1
        columns.append(
            (marked[:, None] & (ranked[:, None] == slot_ids[None, :])).astype(jnp.float32)
        )
    placing = jnp.concatenate(columns, axis=1)
    packed = jnp.einsum("crlij,js->crlis", updated, placing)
    arrivals = []
    for position, shift_by in enumerate(OFFSET_VALUES):
        outgoing = packed[:, :, :, :, position * SHIFT_CAP : (position + 1) * SHIFT_CAP]
        arrivals.append(from_behind(outgoing, "col", shift_by))
    arrived = jnp.concatenate(arrivals, axis=4)
    remeshed = remeshed + jnp.einsum("crlis,js->crlij", arrived, placing)
    keep_here = jnp.sum(
        jnp.where(jnp.arange(cols_count, dtype=jnp.int32) == col_index, keep_blocks, 0)
    ).astype(jnp.float32)
    return remeshed * keep_here


def solution(mesh):
    placed = (P(None, None, "row", "col", None), P(None, None, "row", "col", None), P(), P(), P())
    return jax.shard_map(
        local,
        mesh=mesh,
        in_specs=placed,
        out_specs=P(None, None, "row", "col", None),
        check_vma=False,
    )
```

profile of v0, /device:TPU:110, one launch (start us, length us, event | category | flops | bytes accessed | tf_op | source)
XLA Modules:
  0.0 446.3 jit_solution(11688594146885093595)
XLA Ops:
  5.5 4.4 copy.85
  10.0 7.9 %reshape.1762 = bf16[16,2,18432]{2,1,0:T(2,128)(2,1)} reshape(bf16[384,2,3,8,32]{4,3,2,1,0:T(8,128)(2,1)} %bitcast.373) | data formatting | bytes 2359296
  17.8 7.0 %all-to-all-start = ((bf16[16,2,18432]{2,1,0:T(2,128)(2,1)}), bf16[16,2,18432]{2,1,0:T(2,128)(2,1)S(1)}, u32[]{:S(2)}, u32[]{:S(2)}) async-start(bf16[16,2,18432]{2,1,0:T(2,128)(2,1)} %reshape.1762), calls=%async_computation | async-start | bytes 2359296 | tf_op jit(solution)/shard_map/all_to_all | solution.py:42
  24.9 4.4 copy.88
  29.3 7.8 %reshape.1760 = bf16[16,2,18432]{2,1,0:T(2,128)(2,1)} reshape(bf16[384,2,3,8,32]{4,3,2,1,0:T(8,128)(2,1)} %bitcast.374) | data formatting | bytes 2359296
  40.1 8.3 %all-to-all-start.1 = ((bf16[16,2,18432]{2,1,0:T(2,128)(2,1)}), bf16[16,2,18432]{2,1,0:T(2,128)(2,1)S(1)}, u32[]{:S(2)}, u32[]{:S(2)}) async-start(bf16[16,2,18432]{2,1,0:T(2,128)(2,1)} %reshape.1760), calls=%async_computation.1 | async-start | bytes 2359296 | tf_op jit(solution)/shard_map/all_to_all | solution.py:42
  48.4 7.2 %fusion.47 = (bf16[512,1,768]{2,0,1:T(8,128)(2,1)S(1)}, bf16[512,1,768]{2,0,1:T(8,128)(2,1)S(1)}, bf16[512,1,768]{2,0,1:T(8,128)(2,1)S(1)}) fusion(s32[512]{0:T(512)S(1)} %iota_add_fusion), kind=kLoop, calls=%fused_computation.66 | loop fusion | flops 5111808 | bytes 2361344 | tf_op jit(solution)/shard_map/convert.28
  61.4 7.5 %copy.87 = bf16[3,2,8,16,32,24]{4,3,5,1,2,0:T(8,128)(2,1)} copy(bf16[3,2,8,16,32,24]{4,2,0,1,5,3:T(8,128)(2,1)} %bitcast.375) | data formatting | bytes 2359296 | tf_op jit(solution)/shard_map/all_to_all | solution.py:42
  69.0 7.3 %reshape.1738 = bf16[3,2,8,512,24,1]{3,4,1,2,0,5:T(8,128)(2,1)} reshape(bf16[3,2,8,16,32,24]{4,3,5,1,2,0:T(8,128)(2,1)} %copy.87) | data formatting | bytes 2359296 | tf_op jit(solution)/shard_map/all_to_all | solution.py:42
  76.3 3.9 reshape.1761
  80.1 7.5 %copy.90 = bf16[3,2,8,16,32,24]{4,3,5,1,2,0:T(8,128)(2,1)} copy(bf16[3,2,8,16,32,24]{4,2,0,1,5,3:T(8,128)(2,1)} %bitcast.376) | data formatting | bytes 2359296 | tf_op jit(solution)/shard_map/all_to_all | solution.py:42
  87.7 7.6 %reshape.1740 = bf16[3,2,8,512,24,1]{3,4,1,2,0,5:T(8,128)(2,1)} reshape(bf16[3,2,8,16,32,24]{4,3,5,1,2,0:T(8,128)(2,1)} %copy.90) | data formatting | bytes 2359296 | tf_op jit(solution)/shard_map/all_to_all | solution.py:42
  103.5 4.8 %all-to-all-start.2 = ((bf16[3,2,16,24,768]{4,2,0,1,3:T(8,128)(2,1)}), bf16[3,2,16,24,768]{4,2,0,1,3:T(8,128)(2,1)S(1)}, u32[]{:S(2)}, u32[]{:S(2)}) async-start(bf16[3,2,16,24,768]{4,2,0,1,3:T(8,128)(2,1)} %copy.91), calls=%async_computation.2 | async-start | bytes 7077888 | tf_op jit(solution)/shard_map/all_to_all | solution.py:160
  111.4 8.1 %fusion.52 = (bf16[1,768,1,16,32]{1,4,0,3,2:T(8,128)(2,1)}, bf16[1,768,1,16,32]{1,4,0,3,2:T(8,128)(2,1)}, bf16[1,768,1,16,32]{1,4,0,3,2:T(8,128)(2,1)}) fusion(s32[16,32]{1,0:T(8,128)S(1)} %add_add_fusion), kind=kLoop, calls=%fused_computation.75 | loop fusion | flops 5505024 | bytes 2361344 | tf_op jit(solution)/shard_map/convert.36
  119.6 29.3 %all-to-all-done.2 = bf16[3,2,16,24,768]{4,2,0,1,3:T(8,128)(2,1)S(1)} async-done(((bf16[3,2,16,24,768]{4,2,0,1,3:T(8,128)(2,1)}), bf16[3,2,16,24,768]{4,2,0,1,3:T(8,128)(2,1)S(1)}, u32[]{:S(2)}, u32[]{:S(2)}) %all-to-all-start.2) | async-done | bytes 3538976 | tf_op jit(solution)/shard_map/all_to_all | solution.py:160
  154.8 4.0 copy-done
  158.9 12.8 %fusion.4 = bf16[2,128,6,3,768]{4,1,3,2,0:T(8,128)(2,1)} fusion(bf16[6,3,768,384]{3,2,1,0:T(8,128)(2,1)} %copy-done, bf16[384,1,128]{0,2,1:T(8,128)(2,1)S(1)} %copy-done.9, bf16[384,1,128]{0,2,1:T(8,128)(2,1)S(1)} %copy-done.10), kind=kOutput, calls=%fused_computation.7 | convolution fusion | flops 2721841152 | bytes 17891328 | tf_op jit(solution)/shard_map/eabz,zsl->esabl/dot_general | solution.py:170
  171.7 31.7 %fusion = bf16[6,2,3,8,16,16,32]{6,5,3,2,0,4,1:T(8,128)(2,1)S(1)} fusion(bf16[6,2,3,768,8,16,1,1]{3,5,4,2,0,1,7,6:T(8,128)(2,1)} %bitcast.379, bf16[1,768,1,16,32]{1,4,0,3,2:T(8,128)(2,1)S(1)} %copy-done.8, bf16[1,768,1,16,32]{1,4,0,3,2:T(8,128)(2,1)S(1)} %copy-done.7, bf16[1,768,1,16,32]{1,4,0,3,2:T(8,128)(2,1)S(1)} %copy-done.6), kind=kOutput, calls=%fused_computation.1 | convolution fusion | flops 7262699520 | bytes 14155776 | tf_op jit(solution)/shard_map/eryxab,rxscd->esyacbd/dot_general | solution.py:175
  203.3 7.3 %copy.134 = bf16[6,2,3,8,16,16,32]{6,5,1,2,0,4,3:T(8,128)(2,1)} copy(bf16[6,2,3,8,16,16,32]{6,5,3,2,0,4,1:T(8,128)(2,1)S(1)} %fusion) | data formatting | bytes 9437184 | tf_op jit(solution)/shard_map/reshape | solution.py:178
  210.6 26.2 %reshape.1755 = bf16[6,2,3,128,512]{4,1,2,0,3:T(2,128)(2,1)} reshape(bf16[6,2,3,8,16,16,32]{6,5,1,2,0,4,3:T(8,128)(2,1)} %copy.134) | data formatting | bytes 9437184 | tf_op jit(solution)/shard_map/reshape | solution.py:178
  236.8 10.7 %all-to-all-start.3 = ((bf16[6,2,3,128,512]{4,1,2,0,3:T(2,128)(2,1)}), bf16[6,2,3,128,512]{4,1,2,0,3:T(2,128)(2,1)}, u32[]{:S(2)}, u32[]{:S(2)}) async-start(bf16[6,2,3,128,512]{4,1,2,0,3:T(2,128)(2,1)} %reshape.1755), calls=%async_computation.3 | async-start | bytes 9437184 | tf_op jit(solution)/shard_map/all_to_all | solution.py:179
  252.5 48.7 %all-to-all-done.3 = bf16[6,2,3,128,512]{4,1,2,0,3:T(2,128)(2,1)} async-done(((bf16[6,2,3,128,512]{4,1,2,0,3:T(2,128)(2,1)}), bf16[6,2,3,128,512]{4,1,2,0,3:T(2,128)(2,1)}, u32[]{:S(2)}, u32[]{:S(2)}) %all-to-all-start.3) | async-done | bytes 4718624 | tf_op jit(solution)/shard_map/all_to_all | solution.py:179
  301.2 7.7 %copy.98 = bf16[6,2,128,3,1,512]{5,1,3,2,0,4:T(2,128)(2,1)} copy(bf16[6,2,128,3,1,512]{5,1,3,0,2,4:T(2,128)(2,1)} %bitcast.54) | data formatting | bytes 9437184 | tf_op jit(solution)/shard_map/all_to_all | solution.py:179
  309.0 23.4 %reshape.1721 = bf16[6,2,384,16,32]{4,3,1,2,0:T(8,128)(2,1)} reshape(bf16[6,2,128,3,1,512]{5,1,3,2,0,4:T(2,128)(2,1)} %copy.98) | data formatting | bytes 9437184 | tf_op jit(solution)/shard_map/reshape | solution.py:180
  332.4 22.4 %copy.99 = bf16[6,2,384,16,32]{2,4,1,3,0:T(8,128)(2,1)} copy(bf16[6,2,384,16,32]{4,3,1,2,0:T(8,128)(2,1)} %reshape.1721) | data formatting | bytes 9437184 | tf_op jit(solution)/shard_map/reshape | solution.py:180
  354.8 5.5 %fusion.3 = f32[6,2,16,32,256]{4,3,2,0,1:T(8,128)S(1)} fusion(bf16[6,2,384,16,32]{2,4,1,3,0:T(8,128)(2,1)} %copy.99, bf16[1,384,2,256]{3,1,0,2:T(8,128)(2,1)S(1)} %get-tuple-element.36, bf16[1,384,2,256]{3,1,0,2:T(8,128)(2,1)S(1)} %get-tuple-element.35), kind=kOutput, calls=%fused_computation.6 | convolution fusion | flops 2419064832 | bytes 11796480 | tf_op jit(solution)/shard_map/erqli,rqsj->eslij/dot_general | solution.py:182
  366.6 4.7 %collective-permute-start = (bf16[3,2,16,32,32]{4,3,2,1,0:T(8,128)(2,1)}, bf16[3,2,16,32,32]{4,3,2,1,0:T(8,128)(2,1)}, u32[]{:S(2)}, u32[]{:S(2)}) collective-permute-start(bf16[3,2,16,32,32]{4,3,2,1,0:T(8,128)(2,1)} %get-tuple-element.29), channel_id=1, source_target_pairs={{2,0},{3,1},{4,2},{5,3},{6,4},{7,5},{8,6},{9,7},{10,8},{11,9},{12,... | collective-permute-start | bytes 589832 | tf_op jit(solution)/shard_map/ppermute | solution.py:53
  375.0 4.3 collective-permute-start.2
  382.4 8.4 %collective-permute-done = bf16[3,2,16,32,32]{4,3,2,1,0:T(8,128)(2,1)} collective-permute-done((bf16[3,2,16,32,32]{4,3,2,1,0:T(8,128)(2,1)}, bf16[3,2,16,32,32]{4,3,2,1,0:T(8,128)(2,1)}, u32[]{:S(2)}, u32[]{:S(2)}) %collective-permute-start) | collective-permute-done | bytes 196640 | tf_op jit(solution)/shard_map/ppermute | solution.py:53
  390.8 17.0 %collective-permute-done.1 = bf16[3,2,16,32,32]{4,3,2,1,0:T(8,128)(2,1)} collective-permute-done((bf16[3,2,16,32,32]{4,3,2,1,0:T(8,128)(2,1)}, bf16[3,2,16,32,32]{4,3,2,1,0:T(8,128)(2,1)}, u32[]{:S(2)}, u32[]{:S(2)}) %collective-permute-start.1) | collective-permute-done | bytes 196640 | tf_op jit(solution)/shard_map/ppermute | solution.py:53
  407.8 33.5 %collective-permute-done.2 = bf16[3,2,16,32,32]{4,3,2,1,0:T(8,128)(2,1)} collective-permute-done((bf16[3,2,16,32,32]{4,3,2,1,0:T(8,128)(2,1)}, bf16[3,2,16,32,32]{4,3,2,1,0:T(8,128)(2,1)}, u32[]{:S(2)}, u32[]{:S(2)}) %collective-permute-start.2) | collective-permute-done | bytes 196640 | tf_op jit(solution)/shard_map/ppermute | solution.py:53
  441.3 4.9 %add_multiply_fusion = f32[3,2,16,32,256]{4,3,2,1,0:T(8,128)} fusion(f32[1,2,16,32,256]{4,3,2,1,0:T(8,128)S(1)} %maximum_bitcast_fusion.11, f32[1,2,16,32,256]{4,3,2,1,0:T(8,128)S(1)} %maximum_bitcast_fusion.10, f32[1,2,16,32,256]{4,3,2,1,0:T(8,128)S(1)} %maximum_bitcast_fusion.9, pred[256,128,1,1,1]{1,0,4,3,2:T(32,128)(4,1)S(1)} %add_bitcast_fusion, ...), kind=kOutput, calls=%fused_computation.30 | convolution fusion | flops 208404480 | bytes 7111684 | tf_op jit(solution)/shard_map/crlis,js->crlij/dot_general | solution.py:211
  (106 shorter events, 49.0 us)
Async XLA Ops:
  17.8 22.3 %all-to-all-start = ((bf16[16,2,18432]{2,1,0:T(2,128)(2,1)}), bf16[16,2,18432]{2,1,0:T(2,128)(2,1)S(1)}, u32[]{:S(2)}, u32[]{:S(2)}) async-start(bf16[16,2,18432]{2,1,0:T(2,128)(2,1)} %reshape.1762), calls=%async_computation | async-start | bytes 2359296 | tf_op jit(solution)/shard_map/all_to_all | solution.py:42
  40.1 36.2 %all-to-all-start.1 = ((bf16[16,2,18432]{2,1,0:T(2,128)(2,1)}), bf16[16,2,18432]{2,1,0:T(2,128)(2,1)S(1)}, u32[]{:S(2)}, u32[]{:S(2)}) async-start(bf16[16,2,18432]{2,1,0:T(2,128)(2,1)} %reshape.1760), calls=%async_computation.1 | async-start | bytes 2359296 | tf_op jit(solution)/shard_map/all_to_all | solution.py:42
  87.6 7.6 %copy-start.3 = (bf16[1,512,2,768]{3,1,0,2:T(8,128)(2,1)S(1)}, bf16[1,512,2,768]{3,1,0,2:T(8,128)(2,1)}, u32[]{:S(2)}) copy-start(bf16[1,512,2,768]{3,1,0,2:T(8,128)(2,1)} %get-tuple-element.33) | copy-start | bytes 4718596
  87.7 7.6 %copy-start.4 = (bf16[1,512,2,768]{3,1,0,2:T(8,128)(2,1)S(1)}, bf16[1,512,2,768]{3,1,0,2:T(8,128)(2,1)}, u32[]{:S(2)}) copy-start(bf16[1,512,2,768]{3,1,0,2:T(8,128)(2,1)} %get-tuple-element.34) | copy-start | bytes 4718596
  95.3 3.4 copy-start.5
  103.5 45.3 %all-to-all-start.2 = ((bf16[3,2,16,24,768]{4,2,0,1,3:T(8,128)(2,1)}), bf16[3,2,16,24,768]{4,2,0,1,3:T(8,128)(2,1)S(1)}, u32[]{:S(2)}, u32[]{:S(2)}) async-start(bf16[3,2,16,24,768]{4,2,0,1,3:T(8,128)(2,1)} %copy.91), calls=%async_computation.2 | async-start | bytes 7077888 | tf_op jit(solution)/shard_map/all_to_all | solution.py:160
  148.9 0.9 copy-start.11
  148.9 0.9 copy-start.12
  154.3 4.6 %copy-start.9 = (bf16[384,1,128]{0,2,1:T(8,128)(2,1)S(1)}, bf16[384,1,128]{0,2,1:T(8,128)(2,1)}, u32[]{:S(2)}) copy-start(bf16[384,1,128]{0,2,1:T(8,128)(2,1)} %get-tuple-element.67) | copy-start | bytes 294916
  154.3 4.5 %copy-start.10 = (bf16[384,1,128]{0,2,1:T(8,128)(2,1)S(1)}, bf16[384,1,128]{0,2,1:T(8,128)(2,1)}, u32[]{:S(2)}) copy-start(bf16[384,1,128]{0,2,1:T(8,128)(2,1)} %get-tuple-element.68) | copy-start | bytes 294916
  154.8 4.0 copy-start
  158.9 12.8 %copy-start.6 = (bf16[1,768,1,16,32]{1,4,0,3,2:T(8,128)(2,1)S(1)}, bf16[1,768,1,16,32]{1,4,0,3,2:T(8,128)(2,1)}, u32[]{:S(2)}) copy-start(bf16[1,768,1,16,32]{1,4,0,3,2:T(8,128)(2,1)} %get-tuple-element.39) | copy-start | bytes 2359300
  158.9 12.8 %copy-start.7 = (bf16[1,768,1,16,32]{1,4,0,3,2:T(8,128)(2,1)S(1)}, bf16[1,768,1,16,32]{1,4,0,3,2:T(8,128)(2,1)}, u32[]{:S(2)}) copy-start(bf16[1,768,1,16,32]{1,4,0,3,2:T(8,128)(2,1)} %get-tuple-element.40) | copy-start | bytes 2359300
  158.9 12.8 %copy-start.8 = (bf16[1,768,1,16,32]{1,4,0,3,2:T(8,128)(2,1)S(1)}, bf16[1,768,1,16,32]{1,4,0,3,2:T(8,128)(2,1)}, u32[]{:S(2)}) copy-start(bf16[1,768,1,16,32]{1,4,0,3,2:T(8,128)(2,1)} %get-tuple-element.41) | copy-start | bytes 2359300
  236.8 10.7 %copy-start.13 = (s32[256]{0:T(256)S(1)}, s32[256]{0:T(256)}, u32[]{:S(2)}) copy-start(s32[256]{0:T(256)} %param.7) | copy-start | bytes 3076
  236.8 10.7 %copy-start.14 = (s32[256]{0:T(256)S(1)}, s32[256]{0:T(256)}, u32[]{:S(2)}) copy-start(s32[256]{0:T(256)} %param.8) | copy-start | bytes 3076
  236.8 64.4 %all-to-all-start.3 = ((bf16[6,2,3,128,512]{4,1,2,0,3:T(2,128)(2,1)}), bf16[6,2,3,128,512]{4,1,2,0,3:T(2,128)(2,1)}, u32[]{:S(2)}, u32[]{:S(2)}) async-start(bf16[6,2,3,128,512]{4,1,2,0,3:T(2,128)(2,1)} %reshape.1755), calls=%async_computation.3 | async-start | bytes 9437184 | tf_op jit(solution)/shard_map/all_to_all | solution.py:179
  354.8 5.5 %copy-start.1 = (f32[3,2,16,32,256]{4,3,2,1,0:T(8,128)S(1)}, f32[3,2,16,32,256]{4,3,2,1,0:T(8,128)}, u32[]{:S(2)}) copy-start(f32[3,2,16,32,256]{4,3,2,1,0:T(8,128)} %param.5) | copy-start | bytes 9437188
  354.8 5.5 %copy-start.2 = (f32[3,2,16,32,256]{4,3,2,1,0:T(8,128)S(1)}, f32[3,2,16,32,256]{4,3,2,1,0:T(8,128)}, u32[]{:S(2)}) copy-start(f32[3,2,16,32,256]{4,3,2,1,0:T(8,128)} %param.6) | copy-start | bytes 9437188
  364.2 17.0 %copy-start.15 = (s32[16]{0:T(128)S(1)}, s32[16]{0:T(128)}, u32[]{:S(2)}) copy-start(s32[16]{0:T(128)} %param.9) | copy-start | bytes 196
  366.6 24.2 %collective-permute-start = (bf16[3,2,16,32,32]{4,3,2,1,0:T(8,128)(2,1)}, bf16[3,2,16,32,32]{4,3,2,1,0:T(8,128)(2,1)}, u32[]{:S(2)}, u32[]{:S(2)}) collective-permute-start(bf16[3,2,16,32,32]{4,3,2,1,0:T(8,128)(2,1)} %get-tuple-element.29), channel_id=1, source_target_pairs={{2,0},{3,1},{4,2},{5,3},{6,4},{7,5},{8,6},{9,7},{10,8},{11,9},{12,... | collective-permute-start | bytes 589832 | tf_op jit(solution)/shard_map/ppermute | solution.py:53
  371.3 36.5 %collective-permute-start.1 = (bf16[3,2,16,32,32]{4,3,2,1,0:T(8,128)(2,1)}, bf16[3,2,16,32,32]{4,3,2,1,0:T(8,128)(2,1)}, u32[]{:S(2)}, u32[]{:S(2)}) collective-permute-start(bf16[3,2,16,32,32]{4,3,2,1,0:T(8,128)(2,1)} %get-tuple-element.32), channel_id=1, source_target_pairs={{1,0},{2,1},{3,2},{4,3},{5,4},{6,5},{7,6},{8,7},{9,8},{10,9},{11,1... | collective-permute-start | bytes 589832 | tf_op jit(solution)/shard_map/ppermute | solution.py:53
  375.0 66.3 %collective-permute-start.2 = (bf16[3,2,16,32,32]{4,3,2,1,0:T(8,128)(2,1)}, bf16[3,2,16,32,32]{4,3,2,1,0:T(8,128)(2,1)}, u32[]{:S(2)}, u32[]{:S(2)}) collective-permute-start(bf16[3,2,16,32,32]{4,3,2,1,0:T(8,128)(2,1)} %get-tuple-element.31), channel_id=1, source_target_pairs={{0,1},{1,2},{2,3},{3,4},{4,5},{5,6},{6,7},{7,8},{8,9},{9,10},{10,1... | collective-permute-start | bytes 589832 | tf_op jit(solution)/shard_map/ppermute | solution.py:53
  379.2 62.0 %collective-permute-start.3 = (bf16[3,2,16,32,32]{4,3,2,1,0:T(8,128)(2,1)}, bf16[3,2,16,32,32]{4,3,2,1,0:T(8,128)(2,1)}, u32[]{:S(2)}, u32[]{:S(2)}) collective-permute-start(bf16[3,2,16,32,32]{4,3,2,1,0:T(8,128)(2,1)} %get-tuple-element.30), channel_id=1, source_target_pairs={{0,2},{1,3},{2,4},{3,5},{4,6},{5,7},{6,8},{7,9},{8,10},{9,11},{10,... | collective-permute-start | bytes 589832 | tf_op jit(solution)/shard_map/ppermute | solution.py:53
where the time goes:
time: 454 us; the launch traced here: 446 us
  local copies, waits for them, and re-layouts  160 us (35%)
  waiting for transfers between devices  140 us (31%)
  matrix products  66.1 us (15%)
  starting transfers between devices  45.3 us (10%)
  other arithmetic  33.7 us (7%)
    ppermute x4, waiting for transfers between devices, from_behind(): return lax.ppermute(block, axis, route)  58.9 us
    all_to_all x1, waiting for transfers between devices, local(): lax.all_to_all(arranged, ('row', 'col'), split_axis=3, concat_axis=2, til...  48.7 us
    reshape x2, local copies, waits for them, and re-layouts, local(): gathered = gathered.reshape(6, 2, MY, slab_kz, slab_kx)  45.8 us
    reshape x2, local copies, waits for them, and re-layouts, local(): arranged.reshape(6, 2, y_both, rows_count * cols_count, slab_kz * slab_kx)  33.4 us
    dot_general x1, matrix products, local(): jnp.einsum('eryxab,rxscd->esyacbd', modes_z, x_split, preferred_element_t...  31.7 us
    all_to_all x4, local copies, waits for them, and re-layouts, items_in_groups(): lax.all_to_all(group, axis, split_axis=split_dim, concat_axis=concat_dim,...  29.9 us
    all_to_all x1, waiting for transfers between devices, local(): lax.all_to_all(along_x, 'row', split_axis=3, concat_axis=2, tiled=True)  29.3 us
    unnamed x36, local copies, waits for them, and re-layouts  28.1 us
  transfers between devices with their start and end apart: 8, of which 6 were waited for; matrix products, arithmetic and copies ran while one was open for 13% of the time, Pallas kernels for 0%

commit v1 on v0

v1 whole, which is shorter than its diff:
```python
import math

import jax
import jax.numpy as jnp
import numpy as np
from jax import lax
from jax.experimental import pallas as pl
from jax.experimental.pallas import tpu as pltpu
from jax.sharding import PartitionSpec as P

NX, NY, NZ, NZH = 512, 256, 256, 128
MX, MY, MZ = 768, 384, 384
SHIFT_CAP = 32
ROWS, COLS = 8, 16
DEVICES = ROWS * COLS
PLANES = MY // DEVICES
KZL = NZH // ROWS
KXL = NX // COLS
MODES = KZL * KXL
PRODUCTS = 5

SHEAR_RATE = 40.0
SHEAR_TIME = 0.3
VISCOSITY = 0.0015
TIME_STEP = 0.008
REGISTER_WEIGHT = -153.0 / 128.0
UPDATE_WEIGHT = 8.0 / 15.0
OFFSET_VALUES = (-2, -1, 1, 2)
INVERSE_SCALE = 1.0 / math.sqrt(NX * NY * NZ)
FORWARD_SCALE = math.sqrt(NX * NY * NZ) / (MX * MY * MZ)

F32, BF16 = jnp.float32, jnp.bfloat16
NN = (((1,), (0,)), ((), ()))
NT = (((1,), (1,)), ((), ()))


def dot(a, b, dims=NN):
    return lax.dot_general(a, b, dims, preferred_element_type=F32)


def cos_sin(left, right, period):
    turns = np.mod(np.outer(left, right), period)
    angles = turns.astype(np.float32) * np.float32(2.0 * math.pi / period)
    return np.cos(angles), np.sin(angles)


def tables():
    kx = np.arange(NX) - NX // 2
    ky = np.arange(NY) - NY // 2
    quarter, row, four = np.meshgrid(np.arange(4), np.arange(ROWS), np.arange(4), indexing="ij")
    kz = (row * KZL + four * 4 + quarter).reshape(-1)

    def mixed(re, im, axis):
        out = np.stack([re, im], axis=axis + 1)
        shape = list(re.shape)
        shape[axis] *= 2
        return out.reshape(shape)

    c, s = cos_sin(np.arange(MY), ky, MY)
    y_inv = np.stack([np.concatenate([c, -s], 1), np.concatenate([s, c], 1)])
    c, s = cos_sin(kx, np.arange(MX), MX)
    x_inv = np.concatenate([c, s], 1)
    x_fwd = np.concatenate([c.T, s.T], 0)
    c, s = cos_sin(np.arange(MZ), kz, MZ)
    w = np.where(kz == 0, 1.0, 2.0).astype(np.float32)[None]
    z_inv = np.concatenate([mixed(w * c, -w * s, 1), mixed(-w * s, -w * c, 1)], 1)
    z_fwd = np.concatenate([mixed(c.T, -s.T, 0), mixed(-s.T, -c.T, 0)], 0)
    c, s = cos_sin(ky, np.arange(MY), MY)
    c = c.reshape(NY, PLANES, DEVICES)
    s = s.reshape(NY, PLANES, DEVICES)
    y_fwd = np.concatenate([np.stack([c, s], 2), np.stack([-s, c], 2)], 0)
    y_fwd = y_fwd.reshape(2 * NY, 2 * MY)
    return [t.astype(jnp.bfloat16) for t in (y_inv, x_inv, z_inv, z_fwd, x_fwd, y_fwd)]


def lane_blocks(parts):
    lane = lax.broadcasted_iota(jnp.int32, parts[0].shape, 1)
    low_half = lane < 64
    even = (lane // 32) % 2 == 0
    a, b, c, d = parts
    roll = lambda x, n: pltpu.roll(x, n, 1)
    a, c = jnp.where(low_half, a, roll(c, 64)), jnp.where(low_half, roll(a, 64), c)
    b, d = jnp.where(low_half, b, roll(d, 64)), jnp.where(low_half, roll(b, 64), d)
    a, b = jnp.where(even, a, roll(b, 32)), jnp.where(even, roll(a, 96), b)
    c, d = jnp.where(even, c, roll(d, 32)), jnp.where(even, roll(c, 96), d)
    return a, b, c, d


def y_inverse_kernel(v_ref, t_ref, out_ref, both, grid):
    both[:, :NY] = v_ref[0, 0].astype(BF16)
    both[:, NY:] = v_ref[0, 1].astype(BF16)
    for q in range(PLANES):
        for s in range(2):
            for h in range(2):
                part = dot(t_ref[s, q * DEVICES:(q + 1) * DEVICES, :], both[h * 256:(h + 1) * 256, :], NT)
                for k in range(2):
                    grid[pl.ds((2 * h + k) * 2 + s, DEVICES, stride=8), :] = part[:, k * 128:(k + 1) * 128]
        out_ref[:, q, 0] = grid[...].reshape(DEVICES, 8, 128).astype(BF16)


def middle_kernel(in_ref, xi_ref, zi_ref, zf_ref, xf_ref, out_ref, lines, waves, modes):
    for c in range(3):
        for g in range(4):
            parts = [in_ref[:, 4 * g + k, 0, c].reshape(64, 128).astype(F32) for k in range(4)]
            for k, part in enumerate(lane_blocks(parts)):
                lines[c, k * 64:(k + 1) * 64, g * 128:(g + 1) * 128] = part.astype(BF16)
    for c in range(3):
        for half in range(2):
            waves[c, half * 256:(half + 1) * 256, :] = dot(
                lines[c], xi_ref[:, half * MX:(half + 1) * MX]
            ).astype(BF16)
    for t in range(3):
        cols = slice(t * 256, (t + 1) * 256)
        f0, f1, f2 = [dot(zi_ref[...], waves[c, :, cols]) * INVERSE_SCALE for c in range(3)]
        products = (f0 * f0 - f1 * f1, f0 * f1, f0 * f2, f1 * f2, f2 * f2 - f1 * f1)
        for e, product in enumerate(products):
            both = dot(zf_ref[...], product.astype(BF16)).astype(BF16)
            modes[e, :, cols] = both[:256]
            modes[e, :, slice(MX + t * 256, MX + (t + 1) * 256)] = both[256:]
    for e in range(PRODUCTS):
        out = dot(modes[e], xf_ref[...])
        for g in range(4):
            parts = [out[k * 64:(k + 1) * 64, g * 128:(g + 1) * 128] for k in range(4)]
            for k, part in enumerate(lane_blocks(parts)):
                out_ref[:, 4 * g + k, 0, e] = part.astype(BF16).reshape(ROWS, 8, 128)


def placing_matrix(moved):
    line = lax.broadcasted_iota(jnp.int32, (128, NY), 0)
    which = line // SHIFT_CAP
    value = jnp.where(which < 2, which - 2, which - 1)
    marked = jnp.broadcast_to(moved, (128, NY)) == value
    upto = lax.broadcasted_iota(jnp.int32, (NY, NY), 0) <= lax.broadcasted_iota(jnp.int32, (NY, NY), 1)
    rank = dot(jnp.where(marked, 1.0, 0.0).astype(BF16), jnp.where(upto, 1.0, 0.0).astype(BF16))
    slot = (line % SHIFT_CAP + 1).astype(F32)
    return jnp.where(marked & (rank == slot), 1.0, 0.0).astype(BF16)


def waves_of(kx, ky, kz):
    k1 = kx - SHEAR_TIME * ky
    squared = k1 * k1 + ky * ky + kz * kz
    return k1, squared, 1.0 / jnp.maximum(squared, 1.0)


def update_kernel(in_ref, yf_ref, v_ref, r_ref, off_ref, flag_ref, out_ref, pack_ref, grid, lines, spectra, rates):
    row0 = lax.axis_index("row") * KZL
    col0 = lax.axis_index("col") * KXL - NX // 2
    for e in range(PRODUCTS):
        for q in range(PLANES):
            grid[...] = in_ref[:, q, e].reshape(8 * DEVICES, 128).astype(F32)
            for j in range(4):
                for s in range(2):
                    lines[e, (2 * q + s) * 128:(2 * q + s + 1) * 128, j * 128:(j + 1) * 128] = grid[
                        pl.ds(2 * j + s, DEVICES, stride=8), :
                    ].astype(BF16)
    scale = TIME_STEP * FORWARD_SCALE
    for h in range(2):
        cols = slice(h * 256, (h + 1) * 256)
        for e in range(PRODUCTS):
            spectra[e] = dot(yf_ref[...], lines[e, :, cols])

        def project(b, carry):
            y0 = pl.multiple_of(b * 16, 16)
            shape = (16, 256)
            ky = (lax.broadcasted_iota(jnp.int32, shape, 0) + (y0 - NY // 2)).astype(F32)
            n = lax.broadcasted_iota(jnp.int32, shape, 1)
            kx = (n % KXL + col0).astype(F32)
            kz = (n // KXL + (row0 + h * 8)).astype(F32)
            k1, squared, inv = waves_of(kx, ky, kz)
            for r in range(2):
                part = spectra.at[:, pl.ds((1 - r) * NY + y0, 16), :]
                sign = scale if r == 0 else -scale
                s0, s1, s2, s3, s4 = [part[e] * sign for e in range(PRODUCTS)]
                a0 = k1 * s0 + ky * s1 + kz * s2
                a1 = k1 * s1 + kz * s3
                a2 = k1 * s2 + ky * s3 + kz * s4
                div = (k1 * a0 + ky * a1 + kz * a2) * inv
                rates[r, pl.ds(y0, 16), :] = a0 - k1 * div
                rates[2 + r, pl.ds(y0, 16), :] = a1 - ky * div
                rates[4 + r, pl.ds(y0, 16), :] = a2 - kz * div
            return carry

        lax.fori_loop(0, NY // 16, project, 0)
        for m in range(3):
            for r in range(2):
                out_ref[m, r, cols, :] = rates[2 * m + r].T

    def finish(b, carry):
        n0 = pl.multiple_of(b * KXL, KXL)
        shape = (KXL, NY)
        ky = (lax.broadcasted_iota(jnp.int32, shape, 1) - NY // 2).astype(F32)
        kx = (lax.broadcasted_iota(jnp.int32, shape, 0) + col0).astype(F32)
        kz = (row0 + b).astype(F32)
        k1, squared, inv = waves_of(kx, ky, kz)
        lift = (2.0 * SHEAR_RATE * TIME_STEP) * ky * inv
        damp = (VISCOSITY * TIME_STEP) * squared
        for r in range(2):
            v0 = v_ref[0, r, pl.ds(n0, KXL), :]
            for m, k in enumerate((k1, ky, kz)):
                v = v_ref[m, r, pl.ds(n0, KXL), :]
                rate = out_ref[m, r, pl.ds(n0, KXL), :] + k * lift * v0 - damp * v
                if m == 1:
                    rate = rate - (SHEAR_RATE * TIME_STEP) * v0
                rate = rate + REGISTER_WEIGHT * r_ref[m, r, pl.ds(n0, KXL), :]
                out_ref[m, r, pl.ds(n0, KXL), :] = v + UPDATE_WEIGHT * rate
        return carry

    lax.fori_loop(0, KZL, finish, 0)
    placing = placing_matrix(off_ref[...] * flag_ref[...])
    for m in range(3):
        for r in range(2):
            packed = dot(out_ref[m, r].astype(BF16), placing, NT)
            parts = [packed[k * 128:(k + 1) * 128] for k in range(4)]
            for k, part in enumerate(lane_blocks(parts)):
                pack_ref[k, 2 * m + r] = part.astype(BF16)


def remesh_kernel(u_ref, *rest):
    arrived, (off_ref, flag_ref, keep_ref, out_ref) = rest[:4], rest[4:]
    moved = off_ref[...] * flag_ref[...]
    placing = placing_matrix(moved)
    stays = (moved == 0).astype(F32)
    block = lax.broadcasted_iota(jnp.int32, (1, COLS), 1)
    keep = jnp.sum(jnp.where(block == lax.axis_index("col"), keep_ref[...], 0).astype(F32), axis=1, keepdims=True)
    for m in range(3):
        for r in range(2):
            parts = lane_blocks([a[2 * m + r].astype(F32) for a in arrived])
            for k, part in enumerate(parts):
                rows = slice(k * 128, (k + 1) * 128)
                came = dot(part.astype(BF16), placing)
                out_ref[m, r, rows, :] = (u_ref[m, r, rows, :] * stays + came) * keep


def params(**more):
    return pltpu.CompilerParams(vmem_limit_bytes=60 << 20, **more)


def whole(*shape):
    return pl.BlockSpec(shape, lambda *_: (0,) * len(shape))


def local(velocity, register, offsets, remesh_flag, keep_blocks):
    y_inv, x_inv, z_inv, z_fwd, x_fwd, y_fwd = tables()
    velocity = velocity.reshape(3, 2, MODES, NY)
    register = register.reshape(3, 2, MODES, NY)
    offsets = offsets.reshape(1, NY)
    remesh_flag = remesh_flag.reshape(1, NY)
    keep_blocks = keep_blocks.reshape(1, COLS)

    sent = pl.pallas_call(
        y_inverse_kernel,
        grid=(3,),
        in_specs=[
            pl.BlockSpec((1, 2, MODES, NY), lambda c: (c, 0, 0, 0)),
            whole(2, MY, 2 * NY),
        ],
        out_specs=pl.BlockSpec((DEVICES, PLANES, 1, 8, 128), lambda c: (0, 0, c, 0, 0)),
        out_shape=jax.ShapeDtypeStruct((DEVICES, PLANES, 3, 8, 128), BF16),
        scratch_shapes=[pltpu.VMEM((MODES, 2 * NY), BF16), pltpu.VMEM((8 * DEVICES, 128), F32)],
        compiler_params=params(),
        name="y_inverse",
    )(velocity, y_inv)
    came = lax.all_to_all(sent, ("row", "col"), split_axis=0, concat_axis=0, tiled=True)
    came = came.reshape(ROWS, COLS, PLANES, 3, 8, 128)

    sent = pl.pallas_call(
        middle_kernel,
        grid=(PLANES,),
        in_specs=[
            pl.BlockSpec((ROWS, COLS, 1, 3, 8, 128), lambda q: (0, 0, q, 0, 0, 0)),
            whole(NX, 2 * MX),
            whole(MZ, 512),
            whole(512, MZ),
            whole(2 * MX, NX),
        ],
        out_specs=pl.BlockSpec((ROWS, COLS, 1, PRODUCTS, 8, 128), lambda q: (0, 0, q, 0, 0, 0)),
        out_shape=jax.ShapeDtypeStruct((ROWS, COLS, PLANES, PRODUCTS, 8, 128), BF16),
        scratch_shapes=[
            pltpu.VMEM((3, 256, NX), BF16),
            pltpu.VMEM((3, 512, MX), BF16),
            pltpu.VMEM((PRODUCTS, 256, 2 * MX), BF16),
        ],
        compiler_params=params(),
        name="middle",
    )(came, x_inv, z_inv, z_fwd, x_fwd)
    sent = sent.reshape(DEVICES, PLANES, PRODUCTS, 8, 128)
    came = lax.all_to_all(sent, ("row", "col"), split_axis=0, concat_axis=0, tiled=True)

    vmem = pl.BlockSpec(memory_space=pltpu.VMEM)
    updated, packed = pl.pallas_call(
        update_kernel,
        in_specs=[vmem] * 6,
        out_specs=(vmem, vmem),
        out_shape=(
            jax.ShapeDtypeStruct((3, 2, MODES, NY), F32),
            jax.ShapeDtypeStruct((4, 6, 128, 128), BF16),
        ),
        scratch_shapes=[
            pltpu.VMEM((8 * DEVICES, 128), F32),
            pltpu.VMEM((PRODUCTS, 2 * MY, MODES), BF16),
            pltpu.VMEM((PRODUCTS, 2 * NY, 256), F32),
            pltpu.VMEM((6, NY, 256), F32),
        ],
        compiler_params=params(),
        name="update",
    )(came, y_fwd, velocity, register, offsets, remesh_flag)

    arrived = []
    for place, distance in enumerate(OFFSET_VALUES):
        route = [(i - distance, i) for i in range(COLS) if 0 <= i - distance < COLS]
        arrived.append(lax.ppermute(packed[place], "col", route))

    out = pl.pallas_call(
        remesh_kernel,
        in_specs=[vmem] * 8,
        out_specs=vmem,
        out_shape=jax.ShapeDtypeStruct((3, 2, MODES, NY), F32),
        compiler_params=params(),
        name="remesh",
    )(updated, *arrived, offsets, remesh_flag, keep_blocks)
    return out.reshape(3, 2, KZL, KXL, NY)


def solution(mesh):
    placed = (P(None, None, "row", "col", None), P(None, None, "row", "col", None), P(), P(), P())
    return jax.shard_map(
        local,
        mesh=mesh,
        in_specs=placed,
        out_specs=P(None, None, "row", "col", None),
        check_vma=False,
    )
```

time: 454 us -> 172 us (0.38)
  the two profiles are of different devices: /device:TPU:110 before, /device:TPU:9 now
where the time goes in v1:
time: 172 us; the launch traced here: 169 us
  blocking collectives  96.7 us (56%)
  Pallas kernels  51.7 us (30%)
  starting transfers between devices  13.6 us (8%)
  waiting for transfers between devices  5.03 us (3%)
  local copies, waits for them, and re-layouts  1.96 us (1%)
    all_to_all x2, blocking collectives, local(): lax.all_to_all(sent, ('row', 'col'), split_axis=0, concat_axis=0, tiled=T...  96.7 us
    pallas_call x1, Pallas kernels, local(): pl.pallas_call(middle_kernel, grid=(PLANES,), in_specs=[pl.BlockSpec((ROW...  26 us
    pallas_call x1, Pallas kernels, local(): pl.pallas_call(update_kernel, in_specs=[vmem] * 6, out_specs=(vmem, vmem)...  14.4 us
    ppermute x4, starting transfers between devices, local(): arrived.append(lax.ppermute(packed[place], 'col', route))  13.6 us
    pallas_call x1, Pallas kernels, local(): pl.pallas_call(y_inverse_kernel, grid=(3,), in_specs=[pl.BlockSpec((1, 2,...  6.28 us
    ppermute x4, waiting for transfers between devices, local(): arrived.append(lax.ppermute(packed[place], 'col', route))  5.03 us
    pallas_call x1, Pallas kernels, local(): pl.pallas_call(remesh_kernel, in_specs=[vmem] * 8, out_specs=vmem, out_sh...  5 us
  transfers between devices with their start and end apart: 4, of which 2 were waited for; matrix products, arithmetic and copies ran while one was open for 0% of the time, Pallas kernels for 0%

profile of v1, /device:TPU:9, one launch (start us, length us, event | category | flops | bytes accessed | tf_op | source)
XLA Modules:
  0.0 169.0 jit_solution(17709272320842072078)
XLA Ops:
  0.0 6.3 %y_inverse.1 = bf16[128,3,3,8,128]{4,3,2,1,0:T(8,128)(2,1)} custom-call(f32[3,2,512,256]{3,2,1,0:T(8,128)} %bitcast.17, bf16[2,384,512]{2,1,0:T(8,128)(2,1)} %constant.12.clone.t_ref), custom_call_target="tpu_custom_call" | custom-call | tf_op jit(solution)/shard_map/y_inverse/pallas_call | solution.py:250
  6.3 42.8 %all_to_all.10 = bf16[128,3,3,8,128]{4,3,2,1,0:T(8,128)(2,1)} all-to-all(bf16[128,3,3,8,128]{4,3,2,1,0:T(8,128)(2,1)} %y_inverse.1), channel_id=1, replica_groups=mesh['row'=8,'col'=16] {'row','col'}, dimensions={0} | all-to-all | bytes 4718592 | tf_op jit(solution)/shard_map/all_to_all | solution.py:263
  49.1 26.0 %middle.1 = bf16[8,16,3,5,8,128]{5,4,3,2,1,0:T(8,128)(2,1)} custom-call(bf16[8,16,3,3,8,128]{5,4,3,2,1,0:T(8,128)(2,1)} %bitcast.19, bf16[512,1536]{1,0:T(8,128)(2,1)} %constant.13.clone.xi_ref, bf16[384,512]{1,0:T(8,128)(2,1)} %constant.14.clone.zi_ref, bf16[512,384]{1,0:T(8,128)(2,1)} %constant.15.clone.zf_ref, bf16[1536,512]{1,0:T(8,128)(2,1)} %constant.16.clone.xf_ref), custom_call_target="tpu_custom_call" | custom-call | tf_op jit(solution)/shard_map/middle/pallas_call | solution.py:266
  75.1 53.9 %all_to_all.11.in_ref = bf16[128,3,5,8,128]{4,3,2,1,0:T(8,128)(2,1)} all-to-all(bf16[128,3,5,8,128]{4,3,2,1,0:T(8,128)(2,1)} %bitcast.16), channel_id=1, replica_groups=mesh['row'=8,'col'=16] {'row','col'}, dimensions={0} | all-to-all | bytes 7864320 | tf_op jit(solution)/shard_map/all_to_all | solution.py:287
  129.0 14.4 %update.1 = (f32[3,2,512,256]{3,2,1,0:T(8,128)}, bf16[4,6,128,128]{3,2,1,0:T(8,128)(2,1)}) custom-call(bf16[128,3,5,8,128]{4,3,2,1,0:T(8,128)(2,1)} %all_to_all.11.in_ref, bf16[512,768]{1,0:T(8,128)(2,1)} %constant.17.clone.yf_ref, f32[3,2,512,256]{3,2,1,0:T(8,128)} %bitcast.18, f32[3,2,512,256]{3,2,1,0:T(8,128)} %bitcast.20, s32[1,256]{1,0:T(1,128)} %bitcast.21, ...), custom_call_target="tpu_custom_call" | custom-call | tf_op jit(solution)/shard_map/update/pallas_call | solution.py:290
  143.4 1.3 slice_bitcast_fusion
  144.6 3.2 %collective-permute-start.3 = (bf16[6,128,128]{2,1,0:T(8,128)(2,1)S(1)}, bf16[6,128,128]{2,1,0:T(8,128)(2,1)S(1)}, u32[]{:S(2)}, u32[]{:S(2)}) collective-permute-start(bf16[6,128,128]{2,1,0:T(8,128)(2,1)S(1)} %get-tuple-element.9), channel_id=1, source_target_pairs={{0,2},{1,3},{2,4},{3,5},{4,6},{5,7},{6,8},{7,9},{8,10},{9,11},{10,... | collective-permute-start | bytes 589832 | tf_op jit(solution)/shard_map/ppermute | solution.py:311
  147.9 3.4 %collective-permute-start.2 = (bf16[6,128,128]{2,1,0:T(8,128)(2,1)S(1)}, bf16[6,128,128]{2,1,0:T(8,128)(2,1)S(1)}, u32[]{:S(2)}, u32[]{:S(2)}) collective-permute-start(bf16[6,128,128]{2,1,0:T(8,128)(2,1)S(1)} %get-tuple-element.10), channel_id=1, source_target_pairs={{0,1},{1,2},{2,3},{3,4},{4,5},{5,6},{6,7},{7,8},{8,9},{9,10},{10,1... | collective-permute-start | bytes 589832 | tf_op jit(solution)/shard_map/ppermute | solution.py:311
  151.2 4.0 %collective-permute-start.1 = (bf16[6,128,128]{2,1,0:T(8,128)(2,1)S(1)}, bf16[6,128,128]{2,1,0:T(8,128)(2,1)S(1)}, u32[]{:S(2)}, u32[]{:S(2)}) collective-permute-start(bf16[6,128,128]{2,1,0:T(8,128)(2,1)S(1)} %get-tuple-element.11), channel_id=1, source_target_pairs={{1,0},{2,1},{3,2},{4,3},{5,4},{6,5},{7,6},{8,7},{9,8},{10,9},{11,1... | collective-permute-start | bytes 589832 | tf_op jit(solution)/shard_map/ppermute | solution.py:311
  155.3 3.0 %collective-permute-start = (bf16[6,128,128]{2,1,0:T(8,128)(2,1)S(1)}, bf16[6,128,128]{2,1,0:T(8,128)(2,1)S(1)}, u32[]{:S(2)}, u32[]{:S(2)}) collective-permute-start(bf16[6,128,128]{2,1,0:T(8,128)(2,1)S(1)} %get-tuple-element.12), channel_id=1, source_target_pairs={{2,0},{3,1},{4,2},{5,3},{6,4},{7,5},{8,6},{9,7},{10,8},{11,9},{12,... | collective-permute-start | bytes 589832 | tf_op jit(solution)/shard_map/ppermute | solution.py:311
  158.2 0.0 collective-permute-done.3.rest_3_
  158.2 0.0 copy-start
  158.3 2.3 %collective-permute-done.2.rest_2_ = bf16[6,128,128]{2,1,0:T(8,128)(2,1)S(1)} collective-permute-done((bf16[6,128,128]{2,1,0:T(8,128)(2,1)S(1)}, bf16[6,128,128]{2,1,0:T(8,128)(2,1)S(1)}, u32[]{:S(2)}, u32[]{:S(2)}) %collective-permute-start.2) | collective-permute-done | bytes 196640 | tf_op jit(solution)/shard_map/ppermute | solution.py:311
  160.6 0.0 copy-start.1
  160.6 0.0 collective-permute-done.1.rest_1_
  160.6 0.0 copy-start.2
  160.6 2.7 %collective-permute-done.rest_0_ = bf16[6,128,128]{2,1,0:T(8,128)(2,1)S(1)} collective-permute-done((bf16[6,128,128]{2,1,0:T(8,128)(2,1)S(1)}, bf16[6,128,128]{2,1,0:T(8,128)(2,1)S(1)}, u32[]{:S(2)}, u32[]{:S(2)}) %collective-permute-start) | collective-permute-done | bytes 196640 | tf_op jit(solution)/shard_map/ppermute | solution.py:311
  163.3 0.0 copy-start.3
  163.3 0.0 copy-done
  163.3 0.0 copy-done.1
  163.3 0.0 copy-done.2
  163.3 0.7 copy-done.3
  164.0 5.0 %remesh.1 = f32[3,2,512,256]{3,2,1,0:T(8,128)} custom-call(f32[3,2,512,256]{3,2,1,0:T(8,128)} %get-tuple-element.7.u_ref, bf16[6,128,128]{2,1,0:T(8,128)(2,1)} %copy-done.3, bf16[6,128,128]{2,1,0:T(8,128)(2,1)} %copy-done.2, bf16[6,128,128]{2,1,0:T(8,128)(2,1)} %copy-done.1, bf16[6,128,128]{2,1,0:T(8,128)(2,1)} %copy-done, s32[1,256]{1,0:T(1,128)} %bitcast.22, ...), custom_call_target="tpu_custom_call" | custom-call | tf_op jit(solution)/shard_map/remesh/pallas_call | solution.py:313
Async XLA Ops:
  144.6 13.6 %collective-permute-start.3 = (bf16[6,128,128]{2,1,0:T(8,128)(2,1)S(1)}, bf16[6,128,128]{2,1,0:T(8,128)(2,1)S(1)}, u32[]{:S(2)}, u32[]{:S(2)}) collective-permute-start(bf16[6,128,128]{2,1,0:T(8,128)(2,1)S(1)} %get-tuple-element.9), channel_id=1, source_target_pairs={{0,2},{1,3},{2,4},{3,5},{4,6},{5,7},{6,8},{7,9},{8,10},{9,11},{10,... | collective-permute-start | bytes 589832 | tf_op jit(solution)/shard_map/ppermute | solution.py:311
  147.9 12.7 %collective-permute-start.2 = (bf16[6,128,128]{2,1,0:T(8,128)(2,1)S(1)}, bf16[6,128,128]{2,1,0:T(8,128)(2,1)S(1)}, u32[]{:S(2)}, u32[]{:S(2)}) collective-permute-start(bf16[6,128,128]{2,1,0:T(8,128)(2,1)S(1)} %get-tuple-element.10), channel_id=1, source_target_pairs={{0,1},{1,2},{2,3},{3,4},{4,5},{5,6},{6,7},{7,8},{8,9},{9,10},{10,1... | collective-permute-start | bytes 589832 | tf_op jit(solution)/shard_map/ppermute | solution.py:311
  151.2 9.3 %collective-permute-start.1 = (bf16[6,128,128]{2,1,0:T(8,128)(2,1)S(1)}, bf16[6,128,128]{2,1,0:T(8,128)(2,1)S(1)}, u32[]{:S(2)}, u32[]{:S(2)}) collective-permute-start(bf16[6,128,128]{2,1,0:T(8,128)(2,1)S(1)} %get-tuple-element.11), channel_id=1, source_target_pairs={{1,0},{2,1},{3,2},{4,3},{5,4},{6,5},{7,6},{8,7},{9,8},{10,9},{11,1... | collective-permute-start | bytes 589832 | tf_op jit(solution)/shard_map/ppermute | solution.py:311
  155.3 8.0 %collective-permute-start = (bf16[6,128,128]{2,1,0:T(8,128)(2,1)S(1)}, bf16[6,128,128]{2,1,0:T(8,128)(2,1)S(1)}, u32[]{:S(2)}, u32[]{:S(2)}) collective-permute-start(bf16[6,128,128]{2,1,0:T(8,128)(2,1)S(1)} %get-tuple-element.12), channel_id=1, source_target_pairs={{2,0},{3,1},{4,2},{5,3},{6,4},{7,5},{8,6},{9,7},{10,8},{11,9},{12,... | collective-permute-start | bytes 589832 | tf_op jit(solution)/shard_map/ppermute | solution.py:311
  158.2 5.0 %copy-start = (bf16[6,128,128]{2,1,0:T(8,128)(2,1)}, bf16[6,128,128]{2,1,0:T(8,128)(2,1)S(1)}, u32[]{:S(2)}) copy-start(bf16[6,128,128]{2,1,0:T(8,128)(2,1)S(1)} %collective-permute-done.3.rest_3_) | copy-start | bytes 589828
  160.6 2.7 %copy-start.1 = (bf16[6,128,128]{2,1,0:T(8,128)(2,1)}, bf16[6,128,128]{2,1,0:T(8,128)(2,1)S(1)}, u32[]{:S(2)}) copy-start(bf16[6,128,128]{2,1,0:T(8,128)(2,1)S(1)} %collective-permute-done.2.rest_2_) | copy-start | bytes 589828
  160.6 2.7 %copy-start.2 = (bf16[6,128,128]{2,1,0:T(8,128)(2,1)}, bf16[6,128,128]{2,1,0:T(8,128)(2,1)S(1)}, u32[]{:S(2)}) copy-start(bf16[6,128,128]{2,1,0:T(8,128)(2,1)S(1)} %collective-permute-done.1.rest_1_) | copy-start | bytes 589828
  163.3 0.7 copy-start.3

commit v2 on v1

--- a/solution.py
+++ b/solution.py
@@ -231,6 +231,64 @@
                 out_ref[m, r, rows, :] = (u_ref[m, r, rows, :] * stays + came) * keep
 
 
+def coordinates(device):
+    return device // COLS, lax.rem(device, COLS)
+
+
+def exchange_kernel(in_ref, out_ref, send, recv):
+    row, col = lax.axis_index("row"), lax.axis_index("col")
+    me = row * COLS + col
+    x, core, y, z = row // 2, lax.rem(row, 2), col // 4, lax.rem(col, 4)
+
+    def peer(i):
+        to_row = lax.rem(x + lax.rem(i, 4), 4) * 2 + lax.rem(core + i // 64, 2)
+        to_col = lax.rem(y + lax.rem(i // 4, 4), 4) * 4 + lax.rem(z + lax.rem(i // 16, 4), 4)
+        return to_row, to_col
+
+    barrier = pltpu.get_barrier_semaphore()
+
+    def greet(i, carry):
+        pl.semaphore_signal(barrier, inc=1, device_id=peer(i), device_id_type=pl.DeviceIdType.MESH)
+        return carry
+
+    lax.fori_loop(1, DEVICES, greet, 0)
+    pl.semaphore_wait(barrier, DEVICES - 1)
+    for q in range(PLANES):
+
+        def push(i, carry):
+            to = peer(i)
+            pltpu.make_async_remote_copy(
+                src_ref=in_ref.at[to[0] * COLS + to[1], q],
+                dst_ref=out_ref.at[me, q],
+                send_sem=send.at[q],
+                recv_sem=recv.at[q],
+                device_id=to,
+                device_id_type=pl.DeviceIdType.MESH,
+            ).start()
+            return carry
+
+        lax.fori_loop(1, DEVICES, push, 0)
+    out_ref[me] = in_ref[me]
+    for q in range(PLANES):
+        arrived = out_ref.at[pl.ds(0, DEVICES - 1), q]
+        pltpu.make_async_copy(arrived, arrived, recv.at[q]).wait()
+        gone = in_ref.at[pl.ds(0, DEVICES - 1), q]
+        pltpu.make_async_copy(gone, gone, send.at[q]).wait()
+
+
+def exchange(sent, number):
+    vmem = pl.BlockSpec(memory_space=pltpu.VMEM)
+    return pl.pallas_call(
+        exchange_kernel,
+        in_specs=[vmem],
+        out_specs=vmem,
+        out_shape=jax.ShapeDtypeStruct(sent.shape, sent.dtype),
+        scratch_shapes=[pltpu.SemaphoreType.DMA((PLANES,)), pltpu.SemaphoreType.DMA((PLANES,))],
+        compiler_params=params(collective_id=number, has_side_effects=True),
+        name="exchange",
+    )(sent)
+
+
 def params(**more):
     return pltpu.CompilerParams(vmem_limit_bytes=60 << 20, **more)
 
@@ -260,7 +318,7 @@
         compiler_params=params(),
         name="y_inverse",
     )(velocity, y_inv)
-    came = lax.all_to_all(sent, ("row", "col"), split_axis=0, concat_axis=0, tiled=True)
+    came = exchange(sent, 0)
     came = came.reshape(ROWS, COLS, PLANES, 3, 8, 128)
 
     sent = pl.pallas_call(
@@ -284,7 +342,7 @@
         name="middle",
     )(came, x_inv, z_inv, z_fwd, x_fwd)
     sent = sent.reshape(DEVICES, PLANES, PRODUCTS, 8, 128)
-    came = lax.all_to_all(sent, ("row", "col"), split_axis=0, concat_axis=0, tiled=True)
+    came = exchange(sent, 1)
 
     vmem = pl.BlockSpec(memory_space=pltpu.VMEM)
     updated, packed = pl.pallas_call(

time: 172 us -> 178 us (1.035)
  Pallas kernels: 51.7 us -> 154 us
  blocking collectives: 96.7 us -> 0 us
    pallas_call x0 -> x2, Pallas kernels: none -> 102 us  [exchange(): pl.pallas_call(exchange_kernel, in_specs=[vmem], out_specs=vmem, out_shap...]
    all_to_all x2 -> x0, blocking collectives: 96.7 us -> none  [local(): lax.all_to_all(sent, ('row', 'col'), split_axis=0, concat_axis=0, tiled=T...]
where the time goes in v2:
time: 178 us; the launch traced here: 176 us
  Pallas kernels  154 us (87%)
  starting transfers between devices  13.4 us (8%)
  waiting for transfers between devices  6.2 us (3%)
  local copies, waits for them, and re-layouts  1.96 us (1%)
    pallas_call x2, Pallas kernels, exchange(): pl.pallas_call(exchange_kernel, in_specs=[vmem], out_specs=vmem, out_shap...  102 us
    pallas_call x1, Pallas kernels, local(): pl.pallas_call(middle_kernel, grid=(PLANES,), in_specs=[pl.BlockSpec((ROW...  26 us
    pallas_call x1, Pallas kernels, local(): pl.pallas_call(update_kernel, in_specs=[vmem] * 6, out_specs=(vmem, vmem)...  14.6 us
    ppermute x4, starting transfers between devices, local(): arrived.append(lax.ppermute(packed[place], 'col', route))  13.4 us
    pallas_call x1, Pallas kernels, local(): pl.pallas_call(y_inverse_kernel, grid=(3,), in_specs=[pl.BlockSpec((1, 2,...  6.28 us
    ppermute x4, waiting for transfers between devices, local(): arrived.append(lax.ppermute(packed[place], 'col', route))  6.2 us
    pallas_call x1, Pallas kernels, local(): pl.pallas_call(remesh_kernel, in_specs=[vmem] * 8, out_specs=vmem, out_sh...  5 us
  transfers between devices with their start and end apart: 4, of which 2 were waited for; matrix products, arithmetic and copies ran while one was open for 0% of the time, Pallas kernels for 0%

profile of v2, /device:TPU:9, one launch (start us, length us, event | category | flops | bytes accessed | tf_op | source)
XLA Modules:
  0.0 175.6 jit_solution(1626478151707841028)
XLA Ops:
  0.0 6.3 %y_inverse.1.in_ref = bf16[128,3,3,8,128]{4,3,2,1,0:T(8,128)(2,1)} custom-call(f32[3,2,512,256]{3,2,1,0:T(8,128)} %bitcast.17, bf16[2,384,512]{2,1,0:T(8,128)(2,1)} %constant.12.clone.t_ref), custom_call_target="tpu_custom_call" | custom-call | tf_op jit(solution)/shard_map/y_inverse/pallas_call | solution.py:308
  6.3 43.4 %exchange.2 = bf16[128,3,3,8,128]{4,3,2,1,0:T(8,128)(2,1)} custom-call(bf16[128,3,3,8,128]{4,3,2,1,0:T(8,128)(2,1)} %y_inverse.1.in_ref), custom_call_target="tpu_custom_call" | custom-call | tf_op jit(solution)/shard_map/exchange/pallas_call | solution.py:281
  49.6 26.0 %middle.1 = bf16[8,16,3,5,8,128]{5,4,3,2,1,0:T(8,128)(2,1)} custom-call(bf16[8,16,3,3,8,128]{5,4,3,2,1,0:T(8,128)(2,1)} %bitcast.19, bf16[512,1536]{1,0:T(8,128)(2,1)} %constant.13.clone.xi_ref, bf16[384,512]{1,0:T(8,128)(2,1)} %constant.14.clone.zi_ref, bf16[512,384]{1,0:T(8,128)(2,1)} %constant.15.clone.zf_ref, bf16[1536,512]{1,0:T(8,128)(2,1)} %constant.16.clone.xf_ref), custom_call_target="tpu_custom_call" | custom-call | tf_op jit(solution)/shard_map/middle/pallas_call | solution.py:324
  75.7 58.7 %exchange.3.in_ref = bf16[128,3,5,8,128]{4,3,2,1,0:T(8,128)(2,1)} custom-call(bf16[128,3,5,8,128]{4,3,2,1,0:T(8,128)(2,1)} %bitcast.16), custom_call_target="tpu_custom_call" | custom-call | tf_op jit(solution)/shard_map/exchange/pallas_call | solution.py:281
  134.4 14.6 %update.1 = (f32[3,2,512,256]{3,2,1,0:T(8,128)}, bf16[4,6,128,128]{3,2,1,0:T(8,128)(2,1)}) custom-call(bf16[128,3,5,8,128]{4,3,2,1,0:T(8,128)(2,1)} %exchange.3.in_ref, bf16[512,768]{1,0:T(8,128)(2,1)} %constant.17.clone.yf_ref, f32[3,2,512,256]{3,2,1,0:T(8,128)} %bitcast.18, f32[3,2,512,256]{3,2,1,0:T(8,128)} %bitcast.20, s32[1,256]{1,0:T(1,128)} %bitcast.21, ...), custom_call_target="tpu_custom_call" | custom-call | tf_op jit(solution)/shard_map/update/pallas_call | solution.py:348
  149.0 1.3 slice_bitcast_fusion
  150.3 3.9 %collective-permute-start.3 = (bf16[6,128,128]{2,1,0:T(8,128)(2,1)S(1)}, bf16[6,128,128]{2,1,0:T(8,128)(2,1)S(1)}, u32[]{:S(2)}, u32[]{:S(2)}) collective-permute-start(bf16[6,128,128]{2,1,0:T(8,128)(2,1)S(1)} %get-tuple-element.9), channel_id=1, source_target_pairs={{0,2},{1,3},{2,4},{3,5},{4,6},{5,7},{6,8},{7,9},{8,10},{9,11},{10,... | collective-permute-start | bytes 589832 | tf_op jit(solution)/shard_map/ppermute | solution.py:369
  154.2 2.6 %collective-permute-start.2 = (bf16[6,128,128]{2,1,0:T(8,128)(2,1)S(1)}, bf16[6,128,128]{2,1,0:T(8,128)(2,1)S(1)}, u32[]{:S(2)}, u32[]{:S(2)}) collective-permute-start(bf16[6,128,128]{2,1,0:T(8,128)(2,1)S(1)} %get-tuple-element.10), channel_id=1, source_target_pairs={{0,1},{1,2},{2,3},{3,4},{4,5},{5,6},{6,7},{7,8},{8,9},{9,10},{10,1... | collective-permute-start | bytes 589832 | tf_op jit(solution)/shard_map/ppermute | solution.py:369
  156.8 4.8 %collective-permute-start.1 = (bf16[6,128,128]{2,1,0:T(8,128)(2,1)S(1)}, bf16[6,128,128]{2,1,0:T(8,128)(2,1)S(1)}, u32[]{:S(2)}, u32[]{:S(2)}) collective-permute-start(bf16[6,128,128]{2,1,0:T(8,128)(2,1)S(1)} %get-tuple-element.11), channel_id=1, source_target_pairs={{1,0},{2,1},{3,2},{4,3},{5,4},{6,5},{7,6},{8,7},{9,8},{10,9},{11,1... | collective-permute-start | bytes 589832 | tf_op jit(solution)/shard_map/ppermute | solution.py:369
  161.6 2.1 %collective-permute-start = (bf16[6,128,128]{2,1,0:T(8,128)(2,1)S(1)}, bf16[6,128,128]{2,1,0:T(8,128)(2,1)S(1)}, u32[]{:S(2)}, u32[]{:S(2)}) collective-permute-start(bf16[6,128,128]{2,1,0:T(8,128)(2,1)S(1)} %get-tuple-element.12), channel_id=1, source_target_pairs={{2,0},{3,1},{4,2},{5,3},{6,4},{7,5},{8,6},{9,7},{10,8},{11,9},{12,... | collective-permute-start | bytes 589832 | tf_op jit(solution)/shard_map/ppermute | solution.py:369
  163.7 0.0 collective-permute-done.3.rest_3_
  163.7 0.0 copy-start
  163.7 1.6 collective-permute-done.2.rest_2_
  165.3 0.0 copy-start.1
  165.3 0.0 collective-permute-done.1.rest_1_
  165.3 0.0 copy-start.2
  165.3 4.6 %collective-permute-done.rest_0_ = bf16[6,128,128]{2,1,0:T(8,128)(2,1)S(1)} collective-permute-done((bf16[6,128,128]{2,1,0:T(8,128)(2,1)S(1)}, bf16[6,128,128]{2,1,0:T(8,128)(2,1)S(1)}, u32[]{:S(2)}, u32[]{:S(2)}) %collective-permute-start) | collective-permute-done | bytes 196640 | tf_op jit(solution)/shard_map/ppermute | solution.py:369
  169.9 0.0 copy-start.3
  169.9 0.0 copy-done
  169.9 0.0 copy-done.1
  169.9 0.0 copy-done.2
  169.9 0.7 copy-done.3
  170.6 5.0 %remesh.1 = f32[3,2,512,256]{3,2,1,0:T(8,128)} custom-call(f32[3,2,512,256]{3,2,1,0:T(8,128)} %get-tuple-element.7.u_ref, bf16[6,128,128]{2,1,0:T(8,128)(2,1)} %copy-done.3, bf16[6,128,128]{2,1,0:T(8,128)(2,1)} %copy-done.2, bf16[6,128,128]{2,1,0:T(8,128)(2,1)} %copy-done.1, bf16[6,128,128]{2,1,0:T(8,128)(2,1)} %copy-done, s32[1,256]{1,0:T(1,128)} %bitcast.22, ...), custom_call_target="tpu_custom_call" | custom-call | tf_op jit(solution)/shard_map/remesh/pallas_call | solution.py:371
Async XLA Ops:
  150.3 13.5 %collective-permute-start.3 = (bf16[6,128,128]{2,1,0:T(8,128)(2,1)S(1)}, bf16[6,128,128]{2,1,0:T(8,128)(2,1)S(1)}, u32[]{:S(2)}, u32[]{:S(2)}) collective-permute-start(bf16[6,128,128]{2,1,0:T(8,128)(2,1)S(1)} %get-tuple-element.9), channel_id=1, source_target_pairs={{0,2},{1,3},{2,4},{3,5},{4,6},{5,7},{6,8},{7,9},{8,10},{9,11},{10,... | collective-permute-start | bytes 589832 | tf_op jit(solution)/shard_map/ppermute | solution.py:369
  154.2 11.1 %collective-permute-start.2 = (bf16[6,128,128]{2,1,0:T(8,128)(2,1)S(1)}, bf16[6,128,128]{2,1,0:T(8,128)(2,1)S(1)}, u32[]{:S(2)}, u32[]{:S(2)}) collective-permute-start(bf16[6,128,128]{2,1,0:T(8,128)(2,1)S(1)} %get-tuple-element.10), channel_id=1, source_target_pairs={{0,1},{1,2},{2,3},{3,4},{4,5},{5,6},{6,7},{7,8},{8,9},{9,10},{10,1... | collective-permute-start | bytes 589832 | tf_op jit(solution)/shard_map/ppermute | solution.py:369
  156.8 8.5 %collective-permute-start.1 = (bf16[6,128,128]{2,1,0:T(8,128)(2,1)S(1)}, bf16[6,128,128]{2,1,0:T(8,128)(2,1)S(1)}, u32[]{:S(2)}, u32[]{:S(2)}) collective-permute-start(bf16[6,128,128]{2,1,0:T(8,128)(2,1)S(1)} %get-tuple-element.11), channel_id=1, source_target_pairs={{1,0},{2,1},{3,2},{4,3},{5,4},{6,5},{7,6},{8,7},{9,8},{10,9},{11,1... | collective-permute-start | bytes 589832 | tf_op jit(solution)/shard_map/ppermute | solution.py:369
  161.6 8.3 %collective-permute-start = (bf16[6,128,128]{2,1,0:T(8,128)(2,1)S(1)}, bf16[6,128,128]{2,1,0:T(8,128)(2,1)S(1)}, u32[]{:S(2)}, u32[]{:S(2)}) collective-permute-start(bf16[6,128,128]{2,1,0:T(8,128)(2,1)S(1)} %get-tuple-element.12), channel_id=1, source_target_pairs={{2,0},{3,1},{4,2},{5,3},{6,4},{7,5},{8,6},{9,7},{10,8},{11,9},{12,... | collective-permute-start | bytes 589832 | tf_op jit(solution)/shard_map/ppermute | solution.py:369
  163.7 6.2 %copy-start = (bf16[6,128,128]{2,1,0:T(8,128)(2,1)}, bf16[6,128,128]{2,1,0:T(8,128)(2,1)S(1)}, u32[]{:S(2)}) copy-start(bf16[6,128,128]{2,1,0:T(8,128)(2,1)S(1)} %collective-permute-done.3.rest_3_) | copy-start | bytes 589828
  165.3 4.6 %copy-start.1 = (bf16[6,128,128]{2,1,0:T(8,128)(2,1)}, bf16[6,128,128]{2,1,0:T(8,128)(2,1)S(1)}, u32[]{:S(2)}) copy-start(bf16[6,128,128]{2,1,0:T(8,128)(2,1)S(1)} %collective-permute-done.2.rest_2_) | copy-start | bytes 589828
  165.3 4.6 %copy-start.2 = (bf16[6,128,128]{2,1,0:T(8,128)(2,1)}, bf16[6,128,128]{2,1,0:T(8,128)(2,1)S(1)}, u32[]{:S(2)}) copy-start(bf16[6,128,128]{2,1,0:T(8,128)(2,1)S(1)} %collective-permute-done.1.rest_1_) | copy-start | bytes 589828
  169.9 0.7 copy-start.3

commit v3 on v1

v3 whole, which is shorter than its diff:
```python
import math

import jax
import jax.numpy as jnp
import numpy as np
from jax import lax
from jax.experimental import pallas as pl
from jax.experimental.pallas import tpu as pltpu
from jax.sharding import PartitionSpec as P

NX, NY, NZ, NZH = 512, 256, 256, 128
MX, MY, MZ = 768, 384, 384
SHIFT_CAP = 32
ROWS, COLS = 8, 16
DEVICES = ROWS * COLS
PLANES = MY // DEVICES
KZL = NZH // ROWS
KXL = NX // COLS
MODES = KZL * KXL
PRODUCTS = 5

SHEAR_RATE = 40.0
SHEAR_TIME = 0.3
VISCOSITY = 0.0015
TIME_STEP = 0.008
REGISTER_WEIGHT = -153.0 / 128.0
UPDATE_WEIGHT = 8.0 / 15.0
OFFSET_VALUES = (-2, -1, 1, 2)
INVERSE_SCALE = 1.0 / math.sqrt(NX * NY * NZ)
FORWARD_SCALE = math.sqrt(NX * NY * NZ) / (MX * MY * MZ)

F32, BF16 = jnp.float32, jnp.bfloat16
NN = (((1,), (0,)), ((), ()))
NT = (((1,), (1,)), ((), ()))


def dot(a, b, dims=NN):
    return lax.dot_general(a, b, dims, preferred_element_type=F32)


def cos_sin(left, right, period):
    turns = np.mod(np.outer(left, right), period)
    angles = turns.astype(np.float32) * np.float32(2.0 * math.pi / period)
    return np.cos(angles), np.sin(angles)


def tables():
    kx = np.arange(NX) - NX // 2
    ky = np.arange(NY) - NY // 2
    quarter, row, four = np.meshgrid(np.arange(4), np.arange(ROWS), np.arange(4), indexing="ij")
    kz = (row * KZL + four * 4 + quarter).reshape(-1)

    def mixed(re, im, axis):
        out = np.stack([re, im], axis=axis + 1)
        shape = list(re.shape)
        shape[axis] *= 2
        return out.reshape(shape)

    c, s = cos_sin(np.arange(MY), ky, MY)
    y_inv = np.stack([np.concatenate([c, -s], 1), np.concatenate([s, c], 1)])
    y_inv = y_inv.reshape(2, PLANES, DEVICES, 2 * NY).transpose(1, 0, 2, 3).reshape(PLANES, 2 * DEVICES, 2 * NY)
    c, s = cos_sin(kx, np.arange(MX), MX)
    x_inv = np.concatenate([c, s], 1)
    x_fwd = np.concatenate([c.T, s.T], 0)
    c, s = cos_sin(np.arange(MZ), kz, MZ)
    w = np.where(kz == 0, 1.0, 2.0).astype(np.float32)[None]
    z_inv = np.concatenate([mixed(w * c, -w * s, 1), mixed(-w * s, -w * c, 1)], 1)
    z_fwd = np.concatenate([mixed(c.T, -s.T, 0), mixed(-s.T, -c.T, 0)], 0)
    c, s = cos_sin(ky, np.arange(MY), MY)
    c = c.reshape(NY, PLANES, DEVICES)
    s = s.reshape(NY, PLANES, DEVICES)
    y_fwd = np.concatenate([np.stack([c, s], 2), np.stack([-s, c], 2)], 0)
    y_fwd = y_fwd.reshape(2 * NY, 2 * MY)
    return [t.astype(jnp.bfloat16) for t in (y_inv, x_inv, z_inv, z_fwd, x_fwd, y_fwd)]


def lane_blocks(parts):
    lane = lax.broadcasted_iota(jnp.int32, parts[0].shape, 1)
    low_half = lane < 64
    even = (lane // 32) % 2 == 0
    a, b, c, d = parts
    roll = lambda x, n: pltpu.roll(x, n, 1)
    a, c = jnp.where(low_half, a, roll(c, 64)), jnp.where(low_half, roll(a, 64), c)
    b, d = jnp.where(low_half, b, roll(d, 64)), jnp.where(low_half, roll(b, 64), d)
    a, b = jnp.where(even, a, roll(b, 32)), jnp.where(even, roll(a, 96), b)
    c, d = jnp.where(even, c, roll(d, 32)), jnp.where(even, roll(c, 96), d)
    return a, b, c, d


def placing_matrix(moved):
    line = lax.broadcasted_iota(jnp.int32, (128, NY), 0)
    which = line // SHIFT_CAP
    value = jnp.where(which < 2, which - 2, which - 1)
    marked = jnp.broadcast_to(moved, (128, NY)) == value
    upto = lax.broadcasted_iota(jnp.int32, (NY, NY), 0) <= lax.broadcasted_iota(jnp.int32, (NY, NY), 1)
    rank = dot(jnp.where(marked, 1.0, 0.0).astype(BF16), jnp.where(upto, 1.0, 0.0).astype(BF16))
    slot = (line % SHIFT_CAP + 1).astype(F32)
    return jnp.where(marked & (rank == slot), 1.0, 0.0).astype(BF16)


def waves_of(kx, ky, kz):
    k1 = kx - SHEAR_TIME * ky
    squared = k1 * k1 + ky * ky + kz * kz
    return k1, squared, 1.0 / jnp.maximum(squared, 1.0)


def step_kernel(*refs):
    (v_any, r_any, yi_any, xi_any, zi_any, zf_any, xf_any, yf_any, off_ref, flag_ref, out_ref) = refs[:11]
    (v_ref, r_ref, yi_ref, xi_ref, zi_ref, zf_ref, xf_ref, yf_ref) = refs[11:19]
    (both, grids, send_b, recv_b, lines, waves, modes, send_c, recv_c) = refs[19:28]
    (points, partial, spectra, rates, packs, arrived) = refs[28:34]
    (load_sem, out_b, in_b, out_c, in_c, out_m, in_m) = refs[34:]

    loads = [
        pltpu.make_async_copy(source, target, load_sem.at[k])
        for k, (source, target) in enumerate(
            [
                (yi_any, yi_ref),
                (v_any, v_ref),
                (xi_any, xi_ref),
                (zi_any, zi_ref),
                (zf_any, zf_ref),
                (xf_any, xf_ref),
                (yf_any, yf_ref),
                (r_any, r_ref),
            ]
        )
    ]
    for load in loads:
        load.start()

    row, col = lax.axis_index("row"), lax.axis_index("col")
    me = row * COLS + col
    x, core, y, z = row // 2, lax.rem(row, 2), col // 4, lax.rem(col, 4)
    to_rows = [lax.rem(x + d, 4) * 2 + lax.rem(core + e, 2) for d in range(4) for e in range(2)]

    def all_peers(work):
        def step(t, carry):
            to_col = lax.rem(y + t // 4, 4) * 4 + lax.rem(z + lax.rem(t, 4), 4)
            for to_row in to_rows:
                work(to_row, to_col)
            return carry

        lax.fori_loop(1, COLS, step, 0)
        for to_row in to_rows[1:]:
            work(to_row, col)

    barrier = pltpu.get_barrier_semaphore()
    all_peers(
        lambda to_row, to_col: pl.semaphore_signal(
            barrier, inc=1, device_id=(to_row, to_col), device_id_type=pl.DeviceIdType.MESH
        )
    )

    def push(source, target, out_sem, in_sem):
        def one(to_row, to_col):
            pltpu.make_async_remote_copy(
                src_ref=source.at[to_row * COLS + to_col],
                dst_ref=target.at[me],
                send_sem=out_sem,
                recv_sem=in_sem,
                device_id=(to_row, to_col),
                device_id_type=pl.DeviceIdType.MESH,
            ).start()

        all_peers(one)
        target[me] = source[me]

    def drain(buffer, sem):
        others = buffer.at[pl.ds(0, DEVICES - 1)]
        pltpu.make_async_copy(others, others, sem).wait()

    loads[0].wait()
    loads[1].wait()
    for c in range(3):
        both[c, :, :NY] = v_ref[c, 0].astype(BF16)
        both[c, :, NY:] = v_ref[c, 1].astype(BF16)
    for q in range(PLANES):
        for c in range(3):
            grid = grids.at[(3 * q + c) % 2]
            for h in range(2):
                part = dot(yi_ref[q], both[c, h * 256:(h + 1) * 256, :], NT)
                for k in range(2):
                    for s in range(2):
                        grid[pl.ds((2 * h + k) * 2 + s, DEVICES, stride=8), :] = part[
                            s * DEVICES:(s + 1) * DEVICES, k * 128:(k + 1) * 128
                        ]
            send_b[q, :, c] = grid[...].reshape(DEVICES, 8, 128).astype(BF16)
        if q == 0:
            pl.semaphore_wait(barrier, DEVICES - 1)
        push(send_b.at[q], recv_b.at[q], out_b.at[q], in_b.at[q])

    for load in loads[2:6]:
        load.wait()
    for q in range(PLANES):
        drain(recv_b.at[q], in_b.at[q])
        for c in range(3):
            for g in range(4):
                parts = [
                    jnp.concatenate(
                        [recv_b[q, r * COLS + 4 * g + k, c].astype(F32) for r in range(ROWS)], axis=0
                    )
                    for k in range(4)
                ]
                for k, part in enumerate(lane_blocks(parts)):
                    lines[c, k * 64:(k + 1) * 64, g * 128:(g + 1) * 128] = part.astype(BF16)
        for c in range(3):
            for half in range(2):
                waves[c, half * 256:(half + 1) * 256, :] = dot(
                    lines[c], xi_ref[:, half * MX:(half + 1) * MX]
                ).astype(BF16)
        for t in range(3):
            cols = slice(t * 256, (t + 1) * 256)
            f0, f1, f2 = [dot(zi_ref[...], waves[c, :, cols]) * INVERSE_SCALE for c in range(3)]
            products = (f0 * f0 - f1 * f1, f0 * f1, f0 * f2, f1 * f2, f2 * f2 - f1 * f1)
            for e, product in enumerate(products):
                pair = dot(zf_ref[...], product.astype(BF16)).astype(BF16)
                modes[e, :, cols] = pair[:256]
                modes[e, :, slice(MX + t * 256, MX + (t + 1) * 256)] = pair[256:]
        for e in range(PRODUCTS):
            back = dot(modes[e], xf_ref[...])
            for g in range(4):
                parts = [back[k * 64:(k + 1) * 64, g * 128:(g + 1) * 128] for k in range(4)]
                for k, part in enumerate(lane_blocks(parts)):
                    for r in range(ROWS):
                        send_c[q, r * COLS + 4 * g + k, e] = part[r * 8:(r + 1) * 8].astype(BF16)
        push(send_c.at[q], recv_c.at[q], out_c.at[q], in_c.at[q])

    loads[7].wait()
    loads[6].wait()
    row0 = row * KZL
    col0 = col * KXL - NX // 2

    def prepare(b, carry):
        n0 = pl.multiple_of(b * KXL, KXL)
        shape = (KXL, NY)
        ky = (lax.broadcasted_iota(jnp.int32, shape, 1) - NY // 2).astype(F32)
        kx = (lax.broadcasted_iota(jnp.int32, shape, 0) + col0).astype(F32)
        kz = (row0 + b).astype(F32)
        k1, squared, inv = waves_of(kx, ky, kz)
        lift = (2.0 * SHEAR_RATE * TIME_STEP) * ky * inv
        damp = (VISCOSITY * TIME_STEP) * squared
        for r in range(2):
            v0 = v_ref[0, r, pl.ds(n0, KXL), :]
            for m, k in enumerate((k1, ky, kz)):
                v = v_ref[m, r, pl.ds(n0, KXL), :]
                rate = k * lift * v0 - damp * v
                if m == 1:
                    rate = rate - (SHEAR_RATE * TIME_STEP) * v0
                rate = rate + REGISTER_WEIGHT * r_ref[m, r, pl.ds(n0, KXL), :]
                out_ref[m, r, pl.ds(n0, KXL), :] = v + UPDATE_WEIGHT * rate
        return carry

    lax.fori_loop(0, KZL, prepare, 0)
    moved = off_ref[...] * flag_ref[...]
    placing = placing_matrix(moved)
    stays = (moved == 0).astype(F32)

    for q in range(PLANES):
        drain(recv_c.at[q], in_c.at[q])
        for e in range(PRODUCTS):
            grid = grids.at[(PRODUCTS * q + e) % 2]
            grid[...] = recv_c[q, :, e].reshape(8 * DEVICES, 128).astype(F32)
            for j in range(4):
                for s in range(2):
                    points[e, (2 * q + s) * 128:(2 * q + s + 1) * 128, j * 128:(j + 1) * 128] = grid[
                        pl.ds(2 * j + s, DEVICES, stride=8), :
                    ].astype(BF16)
        if q == 1:
            for e in range(PRODUCTS):
                for h in range(2):
                    partial[h, e] = dot(yf_ref[:, :512], points[e, :512, h * 256:(h + 1) * 256])

    scale = UPDATE_WEIGHT * TIME_STEP * FORWARD_SCALE

    def remesh_copy(h, place):
        shift = OFFSET_VALUES[place]
        return pltpu.make_async_remote_copy(
            src_ref=packs.at[h, place],
            dst_ref=arrived.at[h, place],
            send_sem=out_m.at[h, place],
            recv_sem=in_m.at[h, place],
            device_id=(row, col + shift),
            device_id_type=pl.DeviceIdType.MESH,
        )

    def inside(position):
        return (position >= 0) & (position < COLS)

    for h in range(2):
        cols = slice(h * 256, (h + 1) * 256)
        for e in range(PRODUCTS):
            spectra[e] = partial[h, e] + dot(yf_ref[:, 512:], points[e, 512:, cols])

        def project(b, carry):
            y0 = pl.multiple_of(b * 16, 16)
            shape = (16, 256)
            ky = (lax.broadcasted_iota(jnp.int32, shape, 0) + (y0 - NY // 2)).astype(F32)
            n = lax.broadcasted_iota(jnp.int32, shape, 1)
            kx = (n % KXL + col0).astype(F32)
            kz = (n // KXL + (row0 + h * 8)).astype(F32)
            k1, squared, inv = waves_of(kx, ky, kz)
            for r in range(2):
                sign = scale if r == 0 else -scale
                s0, s1, s2, s3, s4 = [
                    spectra[e, pl.ds((1 - r) * NY + y0, 16), :] * sign for e in range(PRODUCTS)
                ]
                a0 = k1 * s0 + ky * s1 + kz * s2
                a1 = k1 * s1 + kz * s3
                a2 = k1 * s2 + ky * s3 + kz * s4
                div = (k1 * a0 + ky * a1 + kz * a2) * inv
                rates[r, pl.ds(y0, 16), :] = a0 - k1 * div
                rates[2 + r, pl.ds(y0, 16), :] = a1 - ky * div
                rates[4 + r, pl.ds(y0, 16), :] = a2 - kz * div
            return carry

        lax.fori_loop(0, NY // 16, project, 0)
        for m in range(3):
            for r in range(2):
                updated = out_ref[m, r, cols, :] + rates[2 * m + r].T
                out_ref[m, r, cols, :] = updated
                packed = dot(updated.astype(BF16), placing, NT)
                parts = [packed[k * 64:(k + 1) * 64] for k in range(4)]
                for k, part in enumerate(lane_blocks(parts)):
                    packs[h, k, 2 * m + r] = part.astype(BF16)
        for place, shift in enumerate(OFFSET_VALUES):

            @pl.when(inside(col + shift))
            def _():
                remesh_copy(h, place).start()

            @pl.when(jnp.logical_not(inside(col - shift)))
            def _():
                arrived[h, place] = jnp.zeros((6, 64, 128), BF16)

    for h in range(2):
        for place, shift in enumerate(OFFSET_VALUES):

            @pl.when(inside(col - shift))
            def _():
                remesh_copy(h, place).wait_recv()

        for m in range(3):
            for r in range(2):
                parts = lane_blocks([arrived[h, place, 2 * m + r].astype(F32) for place in range(4)])
                for k, part in enumerate(parts):
                    rows = slice(h * 256 + k * 64, h * 256 + (k + 1) * 64)
                    out_ref[m, r, rows, :] = out_ref[m, r, rows, :] * stays + dot(part.astype(BF16), placing)

    for q in range(PLANES):
        drain(send_b.at[q], out_b.at[q])
        drain(send_c.at[q], out_c.at[q])
    for h in range(2):
        for place, shift in enumerate(OFFSET_VALUES):

            @pl.when(inside(col + shift))
            def _():
                remesh_copy(h, place).wait_send()


def local(velocity, register, offsets, remesh_flag, keep_blocks):
    constants = tables()
    velocity = velocity.reshape(3, 2, MODES, NY)
    register = register.reshape(3, 2, MODES, NY)
    anywhere = pl.BlockSpec(memory_space=pl.ANY)
    vmem = pl.BlockSpec(memory_space=pltpu.VMEM)
    out = pl.pallas_call(
        step_kernel,
        in_specs=[anywhere] * 8 + [vmem] * 2,
        out_specs=vmem,
        out_shape=jax.ShapeDtypeStruct((3, 2, MODES, NY), F32),
        scratch_shapes=[
            pltpu.VMEM(velocity.shape, F32),
            pltpu.VMEM(register.shape, F32),
            *[pltpu.VMEM(t.shape, BF16) for t in constants],
            pltpu.VMEM((3, MODES, 2 * NY), BF16),
            pltpu.VMEM((2, 8 * DEVICES, 128), F32),
            pltpu.VMEM((PLANES, DEVICES, 3, 8, 128), BF16),
            pltpu.VMEM((PLANES, DEVICES, 3, 8, 128), BF16),
            pltpu.VMEM((3, 256, NX), BF16),
            pltpu.VMEM((3, 512, MX), BF16),
            pltpu.VMEM((PRODUCTS, 256, 2 * MX), BF16),
            pltpu.VMEM((PLANES, DEVICES, PRODUCTS, 8, 128), BF16),
            pltpu.VMEM((PLANES, DEVICES, PRODUCTS, 8, 128), BF16),
            pltpu.VMEM((PRODUCTS, 2 * MY, MODES), BF16),
            pltpu.VMEM((2, PRODUCTS, 2 * NY, 256), F32),
            pltpu.VMEM((PRODUCTS, 2 * NY, 256), F32),
            pltpu.VMEM((6, NY, 256), F32),
            pltpu.VMEM((2, 4, 6, 64, 128), BF16),
            pltpu.VMEM((2, 4, 6, 64, 128), BF16),
            pltpu.SemaphoreType.DMA((8,)),
            pltpu.SemaphoreType.DMA((PLANES,)),
            pltpu.SemaphoreType.DMA((PLANES,)),
            pltpu.SemaphoreType.DMA((PLANES,)),
            pltpu.SemaphoreType.DMA((PLANES,)),
            pltpu.SemaphoreType.DMA((2, 4)),
            pltpu.SemaphoreType.DMA((2, 4)),
        ],
        compiler_params=pltpu.CompilerParams(
            vmem_limit_bytes=63 << 20, collective_id=0, has_side_effects=True
        ),
        name="step",
    )(velocity, register, *constants, offsets.reshape(1, NY), remesh_flag.reshape(1, NY))
    block = jnp.arange(COLS, dtype=jnp.int32)
    keep = jnp.sum(jnp.where(block == lax.axis_index("col"), keep_blocks, 0)).astype(F32)
    return out.reshape(3, 2, KZL, KXL, NY) * keep


def solution(mesh):
    placed = (P(None, None, "row", "col", None), P(None, None, "row", "col", None), P(), P(), P())
    return jax.shard_map(
        local,
        mesh=mesh,
        in_specs=placed,
        out_specs=P(None, None, "row", "col", None),
        check_vma=False,
    )
```

time: 172 us -> 113 us (0.66); the launches traced: 169 us -> 113 us
  blocking collectives: 96.7 us -> 0 us
  Pallas kernels: 51.7 us -> 107 us
  starting transfers between devices: 13.6 us -> 0 us
  other arithmetic: 0 us -> 5.2 us
  waiting for transfers between devices: 5.03 us -> 0 us
  local copies, waits for them, and re-layouts: 1.96 us -> 0 us
    all_to_all x2 -> x0, blocking collectives: 96.7 us -> none  [local(): lax.all_to_all(sent, ('row', 'col'), split_axis=0, concat_axis=0, tiled=T...]
    pallas_call x4 -> x1, Pallas kernels: 51.7 us -> 107 us  [local(): pl.pallas_call(step_kernel, in_specs=[anywhere] * 8 + [vmem] * 2, out_spe...]
    ppermute x4 -> x0, starting transfers between devices: 13.6 us -> none  [local(): arrived.append(lax.ppermute(packed[place], 'col', route))]
    ppermute x4 -> x0, waiting for transfers between devices: 5.03 us -> none  [local(): arrived.append(lax.ppermute(packed[place], 'col', route))]
    mul x0 -> x1, other arithmetic: none -> 3.91 us  [local(): return out.reshape(3, 2, KZL, KXL, NY) * keep]
  transfers between devices with their start and end apart: 4 -> 0, of which waited for: 2 -> 0; matrix products, arithmetic and copies ran while one was open for 0% -> 0% of each run, Pallas kernels for 0% -> 0%
where the time goes in v3:
time: 113 us
  Pallas kernels  107 us (95%)
  other arithmetic  5.2 us (5%)
    pallas_call x1, Pallas kernels, local(): pl.pallas_call(step_kernel, in_specs=[anywhere] * 8 + [vmem] * 2, out_spe...  107 us
    mul x1, other arithmetic, local(): return out.reshape(3, 2, KZL, KXL, NY) * keep  3.91 us

profile of v3, /device:TPU:9, one launch (start us, length us, event | category | flops | bytes accessed | tf_op | source)
XLA Modules:
  0.0 113.0 jit_solution(14230829842476646800)
XLA Ops:
  0.0 1.3 %fusion = s32[]{:T(128)} fusion(s32[16]{0:T(128)} %param.15, s32[]{:T(128)S(6)} %axis_index.12), kind=kLoop, calls=%fused_computation.2 | loop fusion | flops 47 | bytes 72 | tf_op jit(solution)/shard_map/reduce_sum | solution.py:405
  1.9 107.2 %step.1 = f32[3,2,512,256]{3,2,1,0:T(8,128)} custom-call(f32[3,2,512,256]{3,2,1,0:T(8,128)} %bitcast.5, f32[3,2,512,256]{3,2,1,0:T(8,128)} %bitcast.6, bf16[3,256,512]{2,1,0:T(8,128)(2,1)} %constant.18.clone.refs_2_, bf16[512,1536]{1,0:T(8,128)(2,1)} %constant.19.clone.refs_3_, bf16[384,512]{1,0:T(8,128)(2,1)} %constant.20.clone.refs_4_, ...), custom_call_target="tpu_custom_call" | custom-call | tf_op jit(solution)/shard_map/step/pallas_call | solution.py:367
  109.1 3.9 %broadcast_multiply_fusion = f32[3,2,512,256]{3,2,1,0:T(8,128)} fusion(f32[3,2,512,256]{3,2,1,0:T(8,128)} %step.1, f32[]{:T(128)S(6)} %convert_element_type.3), kind=kLoop, calls=%fused_computation | loop fusion | flops 786432 | bytes 6291460 | tf_op jit(solution)/shard_map/mul | solution.py:406

commit v4 on v3

--- a/solution.py
+++ b/solution.py
@@ -11,6 +11,7 @@
 NX, NY, NZ, NZH = 512, 256, 256, 128
 MX, MY, MZ = 768, 384, 384
 SHIFT_CAP = 32
+VMEM_LIMIT = 52 << 20
 ROWS, COLS = 8, 16
 DEVICES = ROWS * COLS
 PLANES = MY // DEVICES
@@ -74,6 +75,20 @@
     return [t.astype(jnp.bfloat16) for t in (y_inv, x_inv, z_inv, z_fwd, x_fwd, y_fwd)]
 
 
+def peer_order():
+    rng = np.random.RandomState(0)
+    left = [(a, b, c, d) for a in range(4) for b in range(4) for c in range(4) for d in range(2)][1:]
+    left = [left[k] for k in rng.permutation(len(left))]
+    hops = np.array([[0, 0], [1, 0], [1, 1], [0, 1]], np.float64)
+    total, order = np.zeros(6), []
+    while left:
+        tries = [total + np.concatenate([hops[d] for d in o[:3]]) for o in left[:24]]
+        best = int(np.argmin([np.round(t.var(), 9) for t in tries]))
+        total = tries[best]
+        order.append(left.pop(best))
+    return order
+
+
 def lane_blocks(parts):
     lane = lax.broadcasted_iota(jnp.int32, parts[0].shape, 1)
     low_half = lane < 64
@@ -105,45 +120,41 @@
 
 
 def step_kernel(*refs):
-    (v_any, r_any, yi_any, xi_any, zi_any, zf_any, xf_any, yf_any, off_ref, flag_ref, out_ref) = refs[:11]
-    (v_ref, r_ref, yi_ref, xi_ref, zi_ref, zf_ref, xf_ref, yf_ref) = refs[11:19]
-    (both, grids, send_b, recv_b, lines, waves, modes, send_c, recv_c) = refs[19:28]
-    (points, partial, spectra, rates, packs, arrived) = refs[28:34]
-    (load_sem, out_b, in_b, out_c, in_c, out_m, in_m) = refs[34:]
-
-    loads = [
-        pltpu.make_async_copy(source, target, load_sem.at[k])
-        for k, (source, target) in enumerate(
-            [
-                (yi_any, yi_ref),
-                (v_any, v_ref),
-                (xi_any, xi_ref),
-                (zi_any, zi_ref),
-                (zf_any, zf_ref),
-                (xf_any, xf_ref),
-                (yf_any, yf_ref),
-                (r_any, r_ref),
-            ]
-        )
+    (v_any, r_any, yi_any, xi_any, zi_any, zf_any, xf_any, yf_any) = refs[:8]
+    (off_any, flag_any, keep_any, out_ref) = refs[8:12]
+    (v_ref, r_ref, yi_ref, xi_ref, zi_ref, zf_ref, xf_ref, yf_ref) = refs[12:20]
+    (off_ref, flag_ref, keep_ref) = refs[20:23]
+    (both, grids, send_b, recv_b, lines, waves, modes, send_c, recv_c) = refs[23:32]
+    (points, partial, rates, packs, arrived) = refs[32:37]
+    (load_sem, out_b, in_b, out_c, in_c, out_m, in_m) = refs[37:]
+
+    pairs = [
+        (yi_any, yi_ref),
+        (v_any, v_ref),
+        (xi_any, xi_ref),
+        (zi_any, zi_ref),
+        (zf_any, zf_ref),
+        (xf_any, xf_ref),
+        (yf_any, yf_ref),
+        (r_any, r_ref),
+        (off_any, off_ref),
+        (flag_any, flag_ref),
+        (keep_any, keep_ref),
     ]
-    for load in loads:
+    loads = [pltpu.make_async_copy(*pair, load_sem.at[k]) for k, pair in enumerate(pairs)]
+    for load in loads[:2]:
         load.start()
 
     row, col = lax.axis_index("row"), lax.axis_index("col")
     me = row * COLS + col
     x, core, y, z = row // 2, lax.rem(row, 2), col // 4, lax.rem(col, 4)
     to_rows = [lax.rem(x + d, 4) * 2 + lax.rem(core + e, 2) for d in range(4) for e in range(2)]
+    to_cols = [lax.rem(y + d, 4) * 4 + lax.rem(z + e, 4) for d in range(4) for e in range(4)]
+    order = peer_order()
 
     def all_peers(work):
-        def step(t, carry):
-            to_col = lax.rem(y + t // 4, 4) * 4 + lax.rem(z + lax.rem(t, 4), 4)
-            for to_row in to_rows:
-                work(to_row, to_col)
-            return carry
-
-        lax.fori_loop(1, COLS, step, 0)
-        for to_row in to_rows[1:]:
-            work(to_row, col)
+        for dx, dy, dz, dcore in order:
+            work(to_rows[dx * 2 + dcore], to_cols[dy * 4 + dz])
 
     barrier = pltpu.get_barrier_semaphore()
     all_peers(
@@ -170,14 +181,17 @@
         others = buffer.at[pl.ds(0, DEVICES - 1)]
         pltpu.make_async_copy(others, others, sem).wait()
 
+    for load in loads[2:]:
+        load.start()
     loads[0].wait()
     loads[1].wait()
     for c in range(3):
         both[c, :, :NY] = v_ref[c, 0].astype(BF16)
         both[c, :, NY:] = v_ref[c, 1].astype(BF16)
-    for q in range(PLANES):
+
+    def y_inverse(q):
         for c in range(3):
-            grid = grids.at[(3 * q + c) % 2]
+            grid = grids.at[c % 2]
             for h in range(2):
                 part = dot(yi_ref[q], both[c, h * 256:(h + 1) * 256, :], NT)
                 for k in range(2):
@@ -186,13 +200,24 @@
                             s * DEVICES:(s + 1) * DEVICES, k * 128:(k + 1) * 128
                         ]
             send_b[q, :, c] = grid[...].reshape(DEVICES, 8, 128).astype(BF16)
-        if q == 0:
-            pl.semaphore_wait(barrier, DEVICES - 1)
+
+    y_inverse(0)
+    pl.semaphore_wait(barrier, DEVICES - 1)
+
+    def outward(q, carry):
+        @pl.when(q > 0)
+        def _():
+            y_inverse(q)
+
         push(send_b.at[q], recv_b.at[q], out_b.at[q], in_b.at[q])
+        return carry
+
+    lax.fori_loop(0, PLANES, outward, 0)
 
     for load in loads[2:6]:
         load.wait()
-    for q in range(PLANES):
+
+    def middle(q, carry):
         drain(recv_b.at[q], in_b.at[q])
         for c in range(3):
             for g in range(4):
@@ -225,9 +250,12 @@
                     for r in range(ROWS):
                         send_c[q, r * COLS + 4 * g + k, e] = part[r * 8:(r + 1) * 8].astype(BF16)
         push(send_c.at[q], recv_c.at[q], out_c.at[q], in_c.at[q])
-
-    loads[7].wait()
-    loads[6].wait()
+        return carry
+
+    lax.fori_loop(0, PLANES, middle, 0)
+
+    for load in loads[6:]:
+        load.wait()
     row0 = row * KZL
     col0 = col * KXL - NX // 2
 
@@ -254,32 +282,44 @@
     lax.fori_loop(0, KZL, prepare, 0)
     moved = off_ref[...] * flag_ref[...]
     placing = placing_matrix(moved)
-    stays = (moved == 0).astype(F32)
-
-    for q in range(PLANES):
+    block = lax.broadcasted_iota(jnp.int32, (1, COLS), 1)
+    keep = jnp.sum(jnp.where(block == col, keep_ref[...], 0).astype(F32), axis=1, keepdims=True)
+    stays = (moved == 0).astype(F32) * keep
+
+    def gather(q):
         drain(recv_c.at[q], in_c.at[q])
         for e in range(PRODUCTS):
-            grid = grids.at[(PRODUCTS * q + e) % 2]
+            grid = grids.at[e % 2]
             grid[...] = recv_c[q, :, e].reshape(8 * DEVICES, 128).astype(F32)
             for j in range(4):
                 for s in range(2):
-                    points[e, (2 * q + s) * 128:(2 * q + s + 1) * 128, j * 128:(j + 1) * 128] = grid[
+                    points[q, e, s * 128:(s + 1) * 128, j * 128:(j + 1) * 128] = grid[
                         pl.ds(2 * j + s, DEVICES, stride=8), :
                     ].astype(BF16)
-        if q == 1:
-            for e in range(PRODUCTS):
-                for h in range(2):
-                    partial[h, e] = dot(yf_ref[:, :512], points[e, :512, h * 256:(h + 1) * 256])
+
+
+    def early(q, carry):
+        gather(q)
+        return carry
+
+    lax.fori_loop(0, PLANES - 1, early, 0)
+    for e in range(PRODUCTS):
+        for h in range(2):
+            cols = slice(h * 256, (h + 1) * 256)
+            partial[h, e] = dot(yf_ref[:, :256], points[0, e, :, cols]) + dot(
+                yf_ref[:, 256:512], points[1, e, :, cols]
+            )
+    gather(PLANES - 1)
 
     scale = UPDATE_WEIGHT * TIME_STEP * FORWARD_SCALE
 
-    def remesh_copy(h, place):
+    def remesh_copy(w, place):
         shift = OFFSET_VALUES[place]
         return pltpu.make_async_remote_copy(
-            src_ref=packs.at[h, place],
-            dst_ref=arrived.at[h, place],
-            send_sem=out_m.at[h, place],
-            recv_sem=in_m.at[h, place],
+            src_ref=packs.at[w, place],
+            dst_ref=arrived.at[w, place],
+            send_sem=out_m.at[w, place],
+            recv_sem=in_m.at[w, place],
             device_id=(row, col + shift),
             device_id_type=pl.DeviceIdType.MESH,
         )
@@ -287,92 +327,98 @@
     def inside(position):
         return (position >= 0) & (position < COLS)
 
-    for h in range(2):
-        cols = slice(h * 256, (h + 1) * 256)
-        for e in range(PRODUCTS):
-            spectra[e] = partial[h, e] + dot(yf_ref[:, 512:], points[e, 512:, cols])
+    for w in range(4):
+        h, u = w // 2, w % 2
+        if u == 0:
+            for e in range(PRODUCTS):
+                partial[h, e] += dot(yf_ref[:, 512:], points[2, e, :, h * 256:(h + 1) * 256])
 
         def project(b, carry):
-            y0 = pl.multiple_of(b * 16, 16)
-            shape = (16, 256)
+            y0 = pl.multiple_of(b * 32, 32)
+            shape = (32, 128)
             ky = (lax.broadcasted_iota(jnp.int32, shape, 0) + (y0 - NY // 2)).astype(F32)
             n = lax.broadcasted_iota(jnp.int32, shape, 1)
             kx = (n % KXL + col0).astype(F32)
-            kz = (n // KXL + (row0 + h * 8)).astype(F32)
+            kz = (n // KXL + (row0 + w * 4)).astype(F32)
             k1, squared, inv = waves_of(kx, ky, kz)
             for r in range(2):
                 sign = scale if r == 0 else -scale
                 s0, s1, s2, s3, s4 = [
-                    spectra[e, pl.ds((1 - r) * NY + y0, 16), :] * sign for e in range(PRODUCTS)
+                    partial[h, e, pl.ds((1 - r) * NY + y0, 32), u * 128:(u + 1) * 128] * sign
+                    for e in range(PRODUCTS)
                 ]
                 a0 = k1 * s0 + ky * s1 + kz * s2
                 a1 = k1 * s1 + kz * s3
                 a2 = k1 * s2 + ky * s3 + kz * s4
                 div = (k1 * a0 + ky * a1 + kz * a2) * inv
-                rates[r, pl.ds(y0, 16), :] = a0 - k1 * div
-                rates[2 + r, pl.ds(y0, 16), :] = a1 - ky * div
-                rates[4 + r, pl.ds(y0, 16), :] = a2 - kz * div
+                rates[r, pl.ds(y0, 32), :] = a0 - k1 * div
+                rates[2 + r, pl.ds(y0, 32), :] = a1 - ky * div
+                rates[4 + r, pl.ds(y0, 32), :] = a2 - kz * div
             return carry
 
-        lax.fori_loop(0, NY // 16, project, 0)
+        lax.fori_loop(0, NY // 32, project, 0)
+        rows = slice(w * 128, (w + 1) * 128)
         for m in range(3):
             for r in range(2):
-                updated = out_ref[m, r, cols, :] + rates[2 * m + r].T
-                out_ref[m, r, cols, :] = updated
+                updated = out_ref[m, r, rows, :] + rates[2 * m + r].T
+                out_ref[m, r, rows, :] = updated * stays
                 packed = dot(updated.astype(BF16), placing, NT)
-                parts = [packed[k * 64:(k + 1) * 64] for k in range(4)]
+                parts = [packed[k * 32:(k + 1) * 32] for k in range(4)]
                 for k, part in enumerate(lane_blocks(parts)):
-                    packs[h, k, 2 * m + r] = part.astype(BF16)
+                    packs[w, k, 2 * m + r] = part.astype(BF16)
         for place, shift in enumerate(OFFSET_VALUES):
 
             @pl.when(inside(col + shift))
             def _():
-                remesh_copy(h, place).start()
+                remesh_copy(w, place).start()
 
             @pl.when(jnp.logical_not(inside(col - shift)))
             def _():
-                arrived[h, place] = jnp.zeros((6, 64, 128), BF16)
-
-    for h in range(2):
+                arrived[w, place] = jnp.zeros((6, 32, 128), BF16)
+
+    for w in range(4):
         for place, shift in enumerate(OFFSET_VALUES):
 
             @pl.when(inside(col - shift))
             def _():
-                remesh_copy(h, place).wait_recv()
+                remesh_copy(w, place).wait_recv()
 
         for m in range(3):
             for r in range(2):
-                parts = lane_blocks([arrived[h, place, 2 * m + r].astype(F32) for place in range(4)])
-                for k, part in enumerate(parts):
-                    rows = slice(h * 256 + k * 64, h * 256 + (k + 1) * 64)
-                    out_ref[m, r, rows, :] = out_ref[m, r, rows, :] * stays + dot(part.astype(BF16), placing)
+                parts = lane_blocks([arrived[w, place, 2 * m + r].astype(F32) for place in range(4)])
+                part = jnp.concatenate(parts, axis=0).astype(BF16)
+                rows = slice(w * 128, (w + 1) * 128)
+                out_ref[m, r, rows, :] += dot(part, placing) * keep
 
     for q in range(PLANES):
         drain(send_b.at[q], out_b.at[q])
         drain(send_c.at[q], out_c.at[q])
-    for h in range(2):
+    for w in range(4):
         for place, shift in enumerate(OFFSET_VALUES):
 
             @pl.when(inside(col + shift))
             def _():
-                remesh_copy(h, place).wait_send()
+                remesh_copy(w, place).wait_send()
 
 
 def local(velocity, register, offsets, remesh_flag, keep_blocks):
     constants = tables()
     velocity = velocity.reshape(3, 2, MODES, NY)
     register = register.reshape(3, 2, MODES, NY)
-    anywhere = pl.BlockSpec(memory_space=pl.ANY)
+    anywhere = pl.BlockSpec(memory_space=pltpu.HBM)
     vmem = pl.BlockSpec(memory_space=pltpu.VMEM)
     out = pl.pallas_call(
         step_kernel,
-        in_specs=[anywhere] * 8 + [vmem] * 2,
+        in_specs=[anywhere] * 11,
         out_specs=vmem,
-        out_shape=jax.ShapeDtypeStruct((3, 2, MODES, NY), F32),
+        out_shape=pltpu.VMEM((3, 2, MODES, NY), F32),
         scratch_shapes=[
             pltpu.VMEM(velocity.shape, F32),
             pltpu.VMEM(register.shape, F32),
             *[pltpu.VMEM(t.shape, BF16) for t in constants],
+            pltpu.VMEM((1, NY), jnp.int32),
+            pltpu.VMEM((1, NY), jnp.int32),
+            pltpu.VMEM((1, COLS), jnp.int32),
             pltpu.VMEM((3, MODES, 2 * NY), BF16),
             pltpu.VMEM((2, 8 * DEVICES, 128), F32),
             pltpu.VMEM((PLANES, DEVICES, 3, 8, 128), BF16),
@@ -382,28 +428,32 @@
             pltpu.VMEM((PRODUCTS, 256, 2 * MX), BF16),
             pltpu.VMEM((PLANES, DEVICES, PRODUCTS, 8, 128), BF16),
             pltpu.VMEM((PLANES, DEVICES, PRODUCTS, 8, 128), BF16),
-            pltpu.VMEM((PRODUCTS, 2 * MY, MODES), BF16),
+            pltpu.VMEM((PLANES, PRODUCTS, 2 * DEVICES, MODES), BF16),
             pltpu.VMEM((2, PRODUCTS, 2 * NY, 256), F32),
-            pltpu.VMEM((PRODUCTS, 2 * NY, 256), F32),
-            pltpu.VMEM((6, NY, 256), F32),
-            pltpu.VMEM((2, 4, 6, 64, 128), BF16),
-            pltpu.VMEM((2, 4, 6, 64, 128), BF16),
-            pltpu.SemaphoreType.DMA((8,)),
+            pltpu.VMEM((6, NY, 128), F32),
+            pltpu.VMEM((4, 4, 6, 32, 128), BF16),
+            pltpu.VMEM((4, 4, 6, 32, 128), BF16),
+            pltpu.SemaphoreType.DMA((11,)),
             pltpu.SemaphoreType.DMA((PLANES,)),
             pltpu.SemaphoreType.DMA((PLANES,)),
             pltpu.SemaphoreType.DMA((PLANES,)),
             pltpu.SemaphoreType.DMA((PLANES,)),
-            pltpu.SemaphoreType.DMA((2, 4)),
-            pltpu.SemaphoreType.DMA((2, 4)),
+            pltpu.SemaphoreType.DMA((4, 4)),
+            pltpu.SemaphoreType.DMA((4, 4)),
         ],
         compiler_params=pltpu.CompilerParams(
-            vmem_limit_bytes=63 << 20, collective_id=0, has_side_effects=True
+            vmem_limit_bytes=VMEM_LIMIT, collective_id=0, has_side_effects=True
         ),
         name="step",
-    )(velocity, register, *constants, offsets.reshape(1, NY), remesh_flag.reshape(1, NY))
-    block = jnp.arange(COLS, dtype=jnp.int32)
-    keep = jnp.sum(jnp.where(block == lax.axis_index("col"), keep_blocks, 0)).astype(F32)
-    return out.reshape(3, 2, KZL, KXL, NY) * keep
+    )(
+        velocity,
+        register,
+        *constants,
+        offsets.reshape(1, NY),
+        remesh_flag.reshape(1, NY),
+        keep_blocks.reshape(1, COLS),
+    )
+    return out.reshape(3, 2, KZL, KXL, NY)
 
 
 def solution(mesh):

time: 113 us -> 102 us (0.903)
  Pallas kernels: 107 us -> 100 us
  other arithmetic: 5.2 us -> 0 us
  local copies, waits for them, and re-layouts: 0 us -> 1.67 us
    pallas_call x1, Pallas kernels: 107 us -> 100 us  [local(): pl.pallas_call(step_kernel, in_specs=[anywhere] * 11, out_specs=vmem, out...]
    mul x1 -> x0, other arithmetic: 3.91 us -> none  [local(): return out.reshape(3, 2, KZL, KXL, NY) * keep]
    unnamed x0 -> x1, local copies, waits for them, and re-layouts: none -> 1.67 us
    reduce_sum x1 -> x0, other arithmetic: 1.29 us -> none  [local(): jnp.sum(jnp.where(block == lax.axis_index('col'), keep_blocks, 0))]
where the time goes in v4:
time: 102 us
  Pallas kernels  100 us (98%)
  local copies, waits for them, and re-layouts  1.67 us (2%)
    pallas_call x1, Pallas kernels, local(): pl.pallas_call(step_kernel, in_specs=[anywhere] * 11, out_specs=vmem, out...  100 us

profile of v4, /device:TPU:9, one launch (start us, length us, event | category | flops | bytes accessed | tf_op | source)
XLA Modules:
  0.0 101.7 jit_solution(14282212980971487781)
XLA Ops:
  0.0 100.1 %step.1 = f32[3,2,512,256]{3,2,1,0:T(8,128)S(1)} custom-call(f32[3,2,512,256]{3,2,1,0:T(8,128)} %bitcast.7, f32[3,2,512,256]{3,2,1,0:T(8,128)} %bitcast.8, bf16[3,256,512]{2,1,0:T(8,128)(2,1)} %constant.12.clone.refs_2_, bf16[512,1536]{1,0:T(8,128)(2,1)} %constant.13.clone.refs_3_, bf16[384,512]{1,0:T(8,128)(2,1)} %constant.14.clone.refs_4_, ...), custom_call_target="tpu_custom_call" | custom-call | tf_op jit(solution)/shard_map/step/pallas_call | solution.py:410
  100.1 1.7 %copy.13 = f32[3,2,16,32,256]{4,3,2,1,0:T(8,128)} copy(f32[3,2,16,32,256]{4,3,2,1,0:T(8,128)S(1)} %bitcast.6) | data formatting | bytes 6291456

commit v5 on v4

--- a/solution.py
+++ b/solution.py
@@ -19,6 +19,7 @@
 KXL = NX // COLS
 MODES = KZL * KXL
 PRODUCTS = 5
+EARLY_TILES, LATE_TILES = (0, 3), (3, 2)
 
 SHEAR_RATE = 40.0
 SHEAR_TIME = 0.3
@@ -67,6 +68,8 @@
     w = np.where(kz == 0, 1.0, 2.0).astype(np.float32)[None]
     z_inv = np.concatenate([mixed(w * c, -w * s, 1), mixed(-w * s, -w * c, 1)], 1)
     z_fwd = np.concatenate([mixed(c.T, -s.T, 0), mixed(-s.T, -c.T, 0)], 0)
+    swapped = z_fwd.reshape(64, 2, 4, MZ)[:, ::-1].reshape(512, MZ)
+    z_fwd = np.stack([z_fwd, swapped])
     c, s = cos_sin(ky, np.arange(MY), MY)
     c = c.reshape(NY, PLANES, DEVICES)
     s = s.reshape(NY, PLANES, DEVICES)
@@ -129,8 +132,11 @@
     (load_sem, out_b, in_b, out_c, in_c, out_m, in_m) = refs[37:]
 
     pairs = [
-        (yi_any, yi_ref),
-        (v_any, v_ref),
+        (yi_any.at[0], yi_ref.at[0]),
+        (v_any.at[0], v_ref.at[0]),
+        (v_any.at[1], v_ref.at[1]),
+        (v_any.at[2], v_ref.at[2]),
+        (yi_any.at[pl.ds(1, 2)], yi_ref.at[pl.ds(1, 2)]),
         (xi_any, xi_ref),
         (zi_any, zi_ref),
         (zf_any, zf_ref),
@@ -142,7 +148,7 @@
         (keep_any, keep_ref),
     ]
     loads = [pltpu.make_async_copy(*pair, load_sem.at[k]) for k, pair in enumerate(pairs)]
-    for load in loads[:2]:
+    for load in loads[:5]:
         load.start()
 
     row, col = lax.axis_index("row"), lax.axis_index("col")
@@ -163,7 +169,11 @@
         )
     )
 
-    def push(source, target, out_sem, in_sem):
+    def push(source, target, out_sem, in_sem, part=None):
+        if part is not None:
+            source = source.at[:, pl.ds(*part)]
+            target = target.at[:, pl.ds(*part)]
+
         def one(to_row, to_col):
             pltpu.make_async_remote_copy(
                 src_ref=source.at[to_row * COLS + to_col],
@@ -177,20 +187,20 @@
         all_peers(one)
         target[me] = source[me]
 
-    def drain(buffer, sem):
+    def drain(buffer, sem, part=None):
+        if part is not None:
+            buffer = buffer.at[:, pl.ds(*part)]
         others = buffer.at[pl.ds(0, DEVICES - 1)]
         pltpu.make_async_copy(others, others, sem).wait()
 
-    for load in loads[2:]:
+    for load in loads[5:]:
         load.start()
-    loads[0].wait()
-    loads[1].wait()
-    for c in range(3):
-        both[c, :, :NY] = v_ref[c, 0].astype(BF16)
-        both[c, :, NY:] = v_ref[c, 1].astype(BF16)
-
-    def y_inverse(q):
+    def y_inverse(q, first=False):
         for c in range(3):
+            if first:
+                loads[1 + c].wait()
+                both[c, :, :NY] = v_ref[c, 0].astype(BF16)
+                both[c, :, NY:] = v_ref[c, 1].astype(BF16)
             grid = grids.at[c % 2]
             for h in range(2):
                 part = dot(yi_ref[q], both[c, h * 256:(h + 1) * 256, :], NT)
@@ -201,7 +211,9 @@
                         ]
             send_b[q, :, c] = grid[...].reshape(DEVICES, 8, 128).astype(BF16)
 
-    y_inverse(0)
+    loads[0].wait()
+    y_inverse(0, first=True)
+    loads[4].wait()
     pl.semaphore_wait(barrier, DEVICES - 1)
 
     def outward(q, carry):
@@ -214,7 +226,7 @@
 
     lax.fori_loop(0, PLANES, outward, 0)
 
-    for load in loads[2:6]:
+    for load in loads[5:9]:
         load.wait()
 
     def middle(q, carry):
@@ -239,22 +251,44 @@
             f0, f1, f2 = [dot(zi_ref[...], waves[c, :, cols]) * INVERSE_SCALE for c in range(3)]
             products = (f0 * f0 - f1 * f1, f0 * f1, f0 * f2, f1 * f2, f2 * f2 - f1 * f1)
             for e, product in enumerate(products):
-                pair = dot(zf_ref[...], product.astype(BF16)).astype(BF16)
+                pair = dot(zf_ref[e % 2], product.astype(BF16)).astype(BF16)
                 modes[e, :, cols] = pair[:256]
                 modes[e, :, slice(MX + t * 256, MX + (t + 1) * 256)] = pair[256:]
-        for e in range(PRODUCTS):
-            back = dot(modes[e], xf_ref[...])
+        def returned(e, g):
+            return lane_blocks(
+                [back[e % 2][k * 64:(k + 1) * 64, g * 128:(g + 1) * 128] for k in range(4)]
+            )
+
+        def post(tile, device, part):
+            for r in range(ROWS):
+                send_c[q, r * COLS + device, tile] = part[r * 8:(r + 1) * 8].astype(BF16)
+
+        for e in (0, 2):
+            back = [dot(modes[e], xf_ref[...]), dot(modes[e + 1], xf_ref[...])]
+            first = lax.broadcasted_iota(jnp.int32, (64, 128), 0) % 8 < 4
             for g in range(4):
-                parts = [back[k * 64:(k + 1) * 64, g * 128:(g + 1) * 128] for k in range(4)]
-                for k, part in enumerate(lane_blocks(parts)):
-                    for r in range(ROWS):
-                        send_c[q, r * COLS + 4 * g + k, e] = part[r * 8:(r + 1) * 8].astype(BF16)
-        push(send_c.at[q], recv_c.at[q], out_c.at[q], in_c.at[q])
+                for k, (even, odd) in enumerate(zip(returned(0, g), returned(1, g))):
+                    post(e // 2, 4 * g + k, jnp.where(first, even, odd))
+                    post(3 + e // 2, 4 * g + k, jnp.where(first, odd, even))
+        back = [dot(modes[4], xf_ref[...])]
+        for g in range(4):
+            for k, part in enumerate(returned(0, g)):
+                post(2, 4 * g + k, part)
+
+        @pl.when(q < PLANES - 1)
+        def _():
+            push(send_c.at[q], recv_c.at[q], out_c.at[q], in_c.at[q])
+
+        @pl.when(q == PLANES - 1)
+        def _():
+            push(send_c.at[q], recv_c.at[q], out_c.at[q], in_c.at[q], EARLY_TILES)
+            push(send_c.at[q], recv_c.at[q], out_c.at[q + 1], in_c.at[q + 1], LATE_TILES)
+
         return carry
 
     lax.fori_loop(0, PLANES, middle, 0)
 
-    for load in loads[6:]:
+    for load in loads[9:]:
         load.wait()
     row0 = row * KZL
     col0 = col * KXL - NX // 2
@@ -286,20 +320,26 @@
     keep = jnp.sum(jnp.where(block == col, keep_ref[...], 0).astype(F32), axis=1, keepdims=True)
     stays = (moved == 0).astype(F32) * keep
 
-    def gather(q):
+    def tile_row(tile, r):
+        if tile == 2:
+            return 4, r // 2, r % 2
+        half, low = tile // 3, r // 4
+        return 2 * (tile % 3) + (low ^ half), 2 * half + r % 4 // 2, r % 2
+
+    def gather(q, tiles):
+        for tile in tiles:
+            grid = grids.at[tile % 2]
+            grid[...] = recv_c[q, :, tile].reshape(8 * DEVICES, 128).astype(F32)
+            for r in range(8):
+                e, j, s = tile_row(tile, r)
+                points[q, e, s * 128:(s + 1) * 128, j * 128:(j + 1) * 128] = grid[
+                    pl.ds(r, DEVICES, stride=8), :
+                ].astype(BF16)
+
+
+    def early(q, carry):
         drain(recv_c.at[q], in_c.at[q])
-        for e in range(PRODUCTS):
-            grid = grids.at[e % 2]
-            grid[...] = recv_c[q, :, e].reshape(8 * DEVICES, 128).astype(F32)
-            for j in range(4):
-                for s in range(2):
-                    points[q, e, s * 128:(s + 1) * 128, j * 128:(j + 1) * 128] = grid[
-                        pl.ds(2 * j + s, DEVICES, stride=8), :
-                    ].astype(BF16)
-
-
-    def early(q, carry):
-        gather(q)
+        gather(q, range(PRODUCTS))
         return carry
 
     lax.fori_loop(0, PLANES - 1, early, 0)
@@ -309,8 +349,6 @@
             partial[h, e] = dot(yf_ref[:, :256], points[0, e, :, cols]) + dot(
                 yf_ref[:, 256:512], points[1, e, :, cols]
             )
-    gather(PLANES - 1)
-
     scale = UPDATE_WEIGHT * TIME_STEP * FORWARD_SCALE
 
     def remesh_copy(w, place):
@@ -330,6 +368,9 @@
     for w in range(4):
         h, u = w // 2, w % 2
         if u == 0:
+            part = (EARLY_TILES, LATE_TILES)[h]
+            drain(recv_c.at[PLANES - 1], in_c.at[PLANES - 1 + h], part)
+            gather(PLANES - 1, range(part[0], part[0] + part[1]))
             for e in range(PRODUCTS):
                 partial[h, e] += dot(yf_ref[:, 512:], points[2, e, :, h * 256:(h + 1) * 256])
 
@@ -392,7 +433,10 @@
 
     for q in range(PLANES):
         drain(send_b.at[q], out_b.at[q])
-        drain(send_c.at[q], out_c.at[q])
+        if q < PLANES - 1:
+            drain(send_c.at[q], out_c.at[q])
+    for h, part in enumerate((EARLY_TILES, LATE_TILES)):
+        drain(send_c.at[PLANES - 1], out_c.at[PLANES - 1 + h], part)
     for w in range(4):
         for place, shift in enumerate(OFFSET_VALUES):
 
@@ -433,11 +477,11 @@
             pltpu.VMEM((6, NY, 128), F32),
             pltpu.VMEM((4, 4, 6, 32, 128), BF16),
             pltpu.VMEM((4, 4, 6, 32, 128), BF16),
-            pltpu.SemaphoreType.DMA((11,)),
+            pltpu.SemaphoreType.DMA((14,)),
             pltpu.SemaphoreType.DMA((PLANES,)),
             pltpu.SemaphoreType.DMA((PLANES,)),
-            pltpu.SemaphoreType.DMA((PLANES,)),
-            pltpu.SemaphoreType.DMA((PLANES,)),
+            pltpu.SemaphoreType.DMA((PLANES + 1,)),
+            pltpu.SemaphoreType.DMA((PLANES + 1,)),
             pltpu.SemaphoreType.DMA((4, 4)),
             pltpu.SemaphoreType.DMA((4, 4)),
         ],

time: 102 us -> 96.8 us (0.949)
  Pallas kernels: 100 us -> 95 us
    pallas_call x1, Pallas kernels: 100 us -> 95 us  [local(): pl.pallas_call(step_kernel, in_specs=[anywhere] * 11, out_specs=vmem, out...]
where the time goes in v5:
time: 96.8 us; the launch traced here: 96.7 us
  Pallas kernels  95 us (98%)
  local copies, waits for them, and re-layouts  1.67 us (2%)
    pallas_call x1, Pallas kernels, local(): pl.pallas_call(step_kernel, in_specs=[anywhere] * 11, out_specs=vmem, out...  95 us

profile of v5, /device:TPU:9, one launch (start us, length us, event | category | flops | bytes accessed | tf_op | source)
XLA Modules:
  0.0 96.7 jit_solution(9452295450082300542)
XLA Ops:
  0.0 95.0 %step.1 = f32[3,2,512,256]{3,2,1,0:T(8,128)S(1)} custom-call(f32[3,2,512,256]{3,2,1,0:T(8,128)} %bitcast.7, f32[3,2,512,256]{3,2,1,0:T(8,128)} %bitcast.8, bf16[3,256,512]{2,1,0:T(8,128)(2,1)} %constant.12.clone.refs_2_, bf16[512,1536]{1,0:T(8,128)(2,1)} %constant.13.clone.refs_3_, bf16[384,512]{1,0:T(8,128)(2,1)} %constant.14.clone.refs_4_, ...), custom_call_target="tpu_custom_call" | custom-call | tf_op jit(solution)/shard_map/step/pallas_call | solution.py:454
  95.0 1.7 %copy.13 = f32[3,2,16,32,256]{4,3,2,1,0:T(8,128)} copy(f32[3,2,16,32,256]{4,3,2,1,0:T(8,128)S(1)} %bitcast.6) | data formatting | bytes 6291456

commit v6 on v5

--- a/solution.py
+++ b/solution.py
@@ -158,15 +158,18 @@
     to_cols = [lax.rem(y + d, 4) * 4 + lax.rem(z + e, 4) for d in range(4) for e in range(4)]
     order = peer_order()
 
-    def all_peers(work):
-        for dx, dy, dz, dcore in order:
+    far_first = sorted(order, key=lambda o: -sum((0, 1, 2, 1)[d] for d in o[:3]))
+
+    def all_peers(work, peers=order):
+        for dx, dy, dz, dcore in peers:
             work(to_rows[dx * 2 + dcore], to_cols[dy * 4 + dz])
 
     barrier = pltpu.get_barrier_semaphore()
     all_peers(
         lambda to_row, to_col: pl.semaphore_signal(
             barrier, inc=1, device_id=(to_row, to_col), device_id_type=pl.DeviceIdType.MESH
-        )
+        ),
+        far_first,
     )
 
     def push(source, target, out_sem, in_sem, part=None):

time: 96.8 us -> 96.2 us (level)
  no operation moved by 1% of the time
where the time goes in v6:
time: 96.2 us; the launch traced here: 96.1 us
  Pallas kernels  94.4 us (98%)
  local copies, waits for them, and re-layouts  1.67 us (2%)
    pallas_call x1, Pallas kernels, local(): pl.pallas_call(step_kernel, in_specs=[anywhere] * 11, out_specs=vmem, out...  94.4 us

profile of v6, /device:TPU:9, one launch (start us, length us, event | category | flops | bytes accessed | tf_op | source)
XLA Modules:
  0.0 96.1 jit_solution(12878272509375700681)
XLA Ops:
  0.0 94.4 %step.1 = f32[3,2,512,256]{3,2,1,0:T(8,128)S(1)} custom-call(f32[3,2,512,256]{3,2,1,0:T(8,128)} %bitcast.7, f32[3,2,512,256]{3,2,1,0:T(8,128)} %bitcast.8, bf16[3,256,512]{2,1,0:T(8,128)(2,1)} %constant.12.clone.refs_2_, bf16[512,1536]{1,0:T(8,128)(2,1)} %constant.13.clone.refs_3_, bf16[384,512]{1,0:T(8,128)(2,1)} %constant.14.clone.refs_4_, ...), custom_call_target="tpu_custom_call" | custom-call | tf_op jit(solution)/shard_map/step/pallas_call | solution.py:457
  94.4 1.7 %copy.13 = f32[3,2,16,32,256]{4,3,2,1,0:T(8,128)} copy(f32[3,2,16,32,256]{4,3,2,1,0:T(8,128)S(1)} %bitcast.6) | data formatting | bytes 6291456

commit v7 on v6

--- a/solution.py
+++ b/solution.py
@@ -19,7 +19,8 @@
 KXL = NX // COLS
 MODES = KZL * KXL
 PRODUCTS = 5
-EARLY_TILES, LATE_TILES = (0, 3), (3, 2)
+SENT = 4
+EARLY_TILES, LATE_TILES = (0, 2), (2, 2)
 
 SHEAR_RATE = 40.0
 SHEAR_TIME = 0.3
@@ -68,8 +69,6 @@
     w = np.where(kz == 0, 1.0, 2.0).astype(np.float32)[None]
     z_inv = np.concatenate([mixed(w * c, -w * s, 1), mixed(-w * s, -w * c, 1)], 1)
     z_fwd = np.concatenate([mixed(c.T, -s.T, 0), mixed(-s.T, -c.T, 0)], 0)
-    swapped = z_fwd.reshape(64, 2, 4, MZ)[:, ::-1].reshape(512, MZ)
-    z_fwd = np.stack([z_fwd, swapped])
     c, s = cos_sin(ky, np.arange(MY), MY)
     c = c.reshape(NY, PLANES, DEVICES)
     s = s.reshape(NY, PLANES, DEVICES)
@@ -105,6 +104,34 @@
     return a, b, c, d
 
 
+NORM = 1.0 + SHEAR_TIME * SHEAR_TIME
+
+
+def combine(back, k, g):
+    t11, t12, t13, t23, t33 = [
+        back[e, k * 64:(k + 1) * 64, g * 128:(g + 1) * 128] for e in range(PRODUCTS)
+    ]
+    shape = (64, 128)
+    line = lax.broadcasted_iota(jnp.int32, shape, 0)
+    kz = (line // 8 * KZL + line % 8 // 2 * 4 + k).astype(F32)
+    kx = (lax.broadcasted_iota(jnp.int32, shape, 1) + (g * 128 - NX // 2)).astype(F32)
+    a1 = kx * t11 + kz * t13
+    a2 = kx * t12 + kz * t23
+    a3 = kx * t13 + kz * t33
+    b1 = t12 - SHEAR_TIME * t11
+    b2 = -SHEAR_TIME * t12
+    b3 = t23 - SHEAR_TIME * t13
+    q1 = kx * a3 - kz * (a1 + SHEAR_TIME * a2)
+    q2 = kx * b3 - kz * (b1 + SHEAR_TIME * b2)
+    d = b2 - SHEAR_TIME * b1
+    beta = NORM * (kx * a1 + kz * a3) - (kx * kx + kz * kz) * d
+    gamma = NORM * (a2 - SHEAR_TIME * a1) + SHEAR_TIME * kx * d
+    if k == 0 and g == 2:
+        mean = (kx == 0.0) & (kz == 0.0)
+        q1, q2, beta = jnp.where(mean, b1, q1), jnp.where(mean, b2, q2), jnp.where(mean, b3, beta)
+    return q1, q2, beta, gamma
+
+
 def placing_matrix(moved):
     line = lax.broadcasted_iota(jnp.int32, (128, NY), 0)
     which = line // SHIFT_CAP
@@ -128,8 +155,8 @@
     (v_ref, r_ref, yi_ref, xi_ref, zi_ref, zf_ref, xf_ref, yf_ref) = refs[12:20]
     (off_ref, flag_ref, keep_ref) = refs[20:23]
     (both, grids, send_b, recv_b, lines, waves, modes, send_c, recv_c) = refs[23:32]
-    (points, partial, rates, packs, arrived) = refs[32:37]
-    (load_sem, out_b, in_b, out_c, in_c, out_m, in_m) = refs[37:]
+    (points, partial, back, rates, packs, arrived) = refs[32:38]
+    (load_sem, out_b, in_b, out_c, in_c, out_m, in_m) = refs[38:]
 
     pairs = [
         (yi_any.at[0], yi_ref.at[0]),
@@ -254,29 +281,23 @@
             f0, f1, f2 = [dot(zi_ref[...], waves[c, :, cols]) * INVERSE_SCALE for c in range(3)]
             products = (f0 * f0 - f1 * f1, f0 * f1, f0 * f2, f1 * f2, f2 * f2 - f1 * f1)
             for e, product in enumerate(products):
-                pair = dot(zf_ref[e % 2], product.astype(BF16)).astype(BF16)
+                pair = dot(zf_ref[...], product.astype(BF16)).astype(BF16)
                 modes[e, :, cols] = pair[:256]
                 modes[e, :, slice(MX + t * 256, MX + (t + 1) * 256)] = pair[256:]
-        def returned(e, g):
-            return lane_blocks(
-                [back[e % 2][k * 64:(k + 1) * 64, g * 128:(g + 1) * 128] for k in range(4)]
-            )
-
-        def post(tile, device, part):
-            for r in range(ROWS):
-                send_c[q, r * COLS + device, tile] = part[r * 8:(r + 1) * 8].astype(BF16)
-
-        for e in (0, 2):
-            back = [dot(modes[e], xf_ref[...]), dot(modes[e + 1], xf_ref[...])]
-            first = lax.broadcasted_iota(jnp.int32, (64, 128), 0) % 8 < 4
-            for g in range(4):
-                for k, (even, odd) in enumerate(zip(returned(0, g), returned(1, g))):
-                    post(e // 2, 4 * g + k, jnp.where(first, even, odd))
-                    post(3 + e // 2, 4 * g + k, jnp.where(first, odd, even))
-        back = [dot(modes[4], xf_ref[...])]
+        for e in range(PRODUCTS):
+            back[e] = dot(modes[e], xf_ref[...])
+        first = lax.broadcasted_iota(jnp.int32, (64, 128), 0) % 8 < 4
         for g in range(4):
-            for k, part in enumerate(returned(0, g)):
-                post(2, 4 * g + k, part)
+            sums = [combine(back, k, g) for k in range(4)]
+            for f in (0, 2):
+                even = lane_blocks([sums[k][f] for k in range(4)])
+                odd = lane_blocks([sums[k][f + 1] for k in range(4)])
+                for k in range(4):
+                    low = jnp.where(first, even[k], pltpu.roll(odd[k], 4, 0))
+                    high = jnp.where(first, pltpu.roll(even[k], 60, 0), odd[k])
+                    for tile, part in ((f // 2, low), (2 + f // 2, high)):
+                        for r in range(ROWS):
+                            send_c[q, r * COLS + 4 * g + k, tile] = part[r * 8:(r + 1) * 8].astype(BF16)
 
         @pl.when(q < PLANES - 1)
         def _():
@@ -324,10 +345,7 @@
     stays = (moved == 0).astype(F32) * keep
 
     def tile_row(tile, r):
-        if tile == 2:
-            return 4, r // 2, r % 2
-        half, low = tile // 3, r // 4
-        return 2 * (tile % 3) + (low ^ half), 2 * half + r % 4 // 2, r % 2
+        return 2 * (tile % 2) + r // 4, 2 * (tile // 2) + r % 4 // 2, r % 2
 
     def gather(q, tiles):
         for tile in tiles:
@@ -342,11 +360,11 @@
 
     def early(q, carry):
         drain(recv_c.at[q], in_c.at[q])
-        gather(q, range(PRODUCTS))
+        gather(q, range(SENT))
         return carry
 
     lax.fori_loop(0, PLANES - 1, early, 0)
-    for e in range(PRODUCTS):
+    for e in range(SENT):
         for h in range(2):
             cols = slice(h * 256, (h + 1) * 256)
             partial[h, e] = dot(yf_ref[:, :256], points[0, e, :, cols]) + dot(
@@ -374,7 +392,7 @@
             part = (EARLY_TILES, LATE_TILES)[h]
             drain(recv_c.at[PLANES - 1], in_c.at[PLANES - 1 + h], part)
             gather(PLANES - 1, range(part[0], part[0] + part[1]))
-            for e in range(PRODUCTS):
+            for e in range(SENT):
                 partial[h, e] += dot(yf_ref[:, 512:], points[2, e, :, h * 256:(h + 1) * 256])
 
         def project(b, carry):
@@ -385,19 +403,27 @@
             kx = (n % KXL + col0).astype(F32)
             kz = (n // KXL + (row0 + w * 4)).astype(F32)
             k1, squared, inv = waves_of(kx, ky, kz)
+            flat = kx * kx + kz * kz
+            mean = flat == 0.0
+            weight = scale / jnp.where(mean, 1.0, kx * kx + NORM * kz * kz)
+            by_beta = (ky - (SHEAR_TIME / NORM) * kx) * inv * weight
+            by_gamma = (ky * ky - flat * (1.0 / NORM)) * inv * weight
+            c21 = ky * kx + SHEAR_TIME * kz * kz
+            c22 = kz * kz + k1 * kx
+            c23 = kz * (ky - SHEAR_TIME * k1)
+            alone = jnp.where(mean, ky * scale, 0.0)
             for r in range(2):
-                sign = scale if r == 0 else -scale
-                s0, s1, s2, s3, s4 = [
-                    partial[h, e, pl.ds((1 - r) * NY + y0, 32), u * 128:(u + 1) * 128] * sign
-                    for e in range(PRODUCTS)
+                q1, q2, beta, gamma = [
+                    partial[h, e, pl.ds((1 - r) * NY + y0, 32), u * 128:(u + 1) * 128] for e in range(SENT)
                 ]
-                a0 = k1 * s0 + ky * s1 + kz * s2
-                a1 = k1 * s1 + kz * s3
-                a2 = k1 * s2 + ky * s3 + kz * s4
-                div = (k1 * a0 + ky * a1 + kz * a2) * inv
-                rates[r, pl.ds(y0, 32), :] = a0 - k1 * div
-                rates[2 + r, pl.ds(y0, 32), :] = a1 - ky * div
-                rates[4 + r, pl.ds(y0, 32), :] = a2 - kz * div
+                p1 = (q1 + ky * q2) * weight
+                p2 = by_beta * beta + by_gamma * gamma
+                across = (q2 - SHEAR_TIME * q1) * (1.0 / NORM)
+                n1 = c21 * p2 - kz * p1 + alone * (q1 + SHEAR_TIME * across)
+                n2 = alone * (q2 - across) - c22 * p2 - SHEAR_TIME * kz * p1
+                n3 = c23 * p2 + kx * p1 + alone * beta
+                for m, part in enumerate((n1, n2, n3)):
+                    rates[2 * m + r, pl.ds(y0, 32), :] = part if r == 0 else -part
             return carry
 
         lax.fori_loop(0, NY // 32, project, 0)
@@ -473,10 +499,11 @@
             pltpu.VMEM((3, 256, NX), BF16),
             pltpu.VMEM((3, 512, MX), BF16),
             pltpu.VMEM((PRODUCTS, 256, 2 * MX), BF16),
-            pltpu.VMEM((PLANES, DEVICES, PRODUCTS, 8, 128), BF16),
-            pltpu.VMEM((PLANES, DEVICES, PRODUCTS, 8, 128), BF16),
-            pltpu.VMEM((PLANES, PRODUCTS, 2 * DEVICES, MODES), BF16),
-            pltpu.VMEM((2, PRODUCTS, 2 * NY, 256), F32),
+            pltpu.VMEM((PLANES, DEVICES, SENT, 8, 128), BF16),
+            pltpu.VMEM((PLANES, DEVICES, SENT, 8, 128), BF16),
+            pltpu.VMEM((PLANES, SENT, 2 * DEVICES, MODES), BF16),
+            pltpu.VMEM((2, SENT, 2 * NY, 256), F32),
+            pltpu.VMEM((PRODUCTS, 256, NX), F32),
             pltpu.VMEM((6, NY, 128), F32),
             pltpu.VMEM((4, 4, 6, 32, 128), BF16),
             pltpu.VMEM((4, 4, 6, 32, 128), BF16),

time: 96.2 us -> 88.1 us (0.916)
  Pallas kernels: 94.4 us -> 85.8 us
    pallas_call x1, Pallas kernels: 94.4 us -> 85.8 us  [local(): pl.pallas_call(step_kernel, in_specs=[anywhere] * 11, out_specs=vmem, out...]
where the time goes in v7:
time: 88.1 us; the launch traced here: 87.5 us
  Pallas kernels  85.8 us (97%)
  local copies, waits for them, and re-layouts  1.67 us (2%)
    pallas_call x1, Pallas kernels, local(): pl.pallas_call(step_kernel, in_specs=[anywhere] * 11, out_specs=vmem, out...  85.8 us

profile of v7, /device:TPU:9, one launch (start us, length us, event | category | flops | bytes accessed | tf_op | source)
XLA Modules:
  0.0 87.5 jit_solution(11730901159450264059)
XLA Ops:
  0.0 85.8 %step.1 = f32[3,2,512,256]{3,2,1,0:T(8,128)S(1)} custom-call(f32[3,2,512,256]{3,2,1,0:T(8,128)} %bitcast.7, f32[3,2,512,256]{3,2,1,0:T(8,128)} %bitcast.8, bf16[3,256,512]{2,1,0:T(8,128)(2,1)} %constant.12.clone.refs_2_, bf16[512,1536]{1,0:T(8,128)(2,1)} %constant.13.clone.refs_3_, bf16[384,512]{1,0:T(8,128)(2,1)} %constant.14.clone.refs_4_, ...), custom_call_target="tpu_custom_call" | custom-call | tf_op jit(solution)/shard_map/step/pallas_call | solution.py:483
  85.8 1.7 %copy.13 = f32[3,2,16,32,256]{4,3,2,1,0:T(8,128)} copy(f32[3,2,16,32,256]{4,3,2,1,0:T(8,128)S(1)} %bitcast.6) | data formatting | bytes 6291456

commit v8 on v7

--- a/solution.py
+++ b/solution.py
@@ -446,26 +446,27 @@
             def _():
                 arrived[w, place] = jnp.zeros((6, 32, 128), BF16)
 
-    for w in range(4):
-        for place, shift in enumerate(OFFSET_VALUES):
-
-            @pl.when(inside(col - shift))
-            def _():
-                remesh_copy(w, place).wait_recv()
-
-        for m in range(3):
-            for r in range(2):
-                parts = lane_blocks([arrived[w, place, 2 * m + r].astype(F32) for place in range(4)])
-                part = jnp.concatenate(parts, axis=0).astype(BF16)
-                rows = slice(w * 128, (w + 1) * 128)
-                out_ref[m, r, rows, :] += dot(part, placing) * keep
-
     for q in range(PLANES):
         drain(send_b.at[q], out_b.at[q])
         if q < PLANES - 1:
             drain(send_c.at[q], out_c.at[q])
     for h, part in enumerate((EARLY_TILES, LATE_TILES)):
         drain(send_c.at[PLANES - 1], out_c.at[PLANES - 1 + h], part)
+    kept = (placing.astype(F32) * keep).astype(BF16)
+    for w in range(4):
+        for place, shift in enumerate(OFFSET_VALUES):
+
+            @pl.when(inside(col - shift))
+            def _():
+                remesh_copy(w, place).wait_recv()
+
+        for m in range(3):
+            for r in range(2):
+                parts = lane_blocks([arrived[w, place, 2 * m + r].astype(F32) for place in range(4)])
+                part = jnp.concatenate(parts, axis=0).astype(BF16)
+                rows = slice(w * 128, (w + 1) * 128)
+                out_ref[m, r, rows, :] += dot(part, kept)
+
     for w in range(4):
         for place, shift in enumerate(OFFSET_VALUES):
 

time: 88.1 us -> 88.1 us (level)
  no operation moved by 1% of the time
where the time goes in v8:
time: 88.1 us; the launch traced here: 87.5 us
  Pallas kernels  85.8 us (97%)
  local copies, waits for them, and re-layouts  1.67 us (2%)
    pallas_call x1, Pallas kernels, local(): pl.pallas_call(step_kernel, in_specs=[anywhere] * 11, out_specs=vmem, out...  85.8 us

profile of v8, /device:TPU:9, one launch (start us, length us, event | category | flops | bytes accessed | tf_op | source)
XLA Modules:
  0.0 87.5 jit_solution(14814875790501282151)
XLA Ops:
  0.0 85.8 %step.1 = f32[3,2,512,256]{3,2,1,0:T(8,128)S(1)} custom-call(f32[3,2,512,256]{3,2,1,0:T(8,128)} %bitcast.7, f32[3,2,512,256]{3,2,1,0:T(8,128)} %bitcast.8, bf16[3,256,512]{2,1,0:T(8,128)(2,1)} %constant.12.clone.refs_2_, bf16[512,1536]{1,0:T(8,128)(2,1)} %constant.13.clone.refs_3_, bf16[384,512]{1,0:T(8,128)(2,1)} %constant.14.clone.refs_4_, ...), custom_call_target="tpu_custom_call" | custom-call | tf_op jit(solution)/shard_map/step/pallas_call | solution.py:484
  85.8 1.7 %copy.13 = f32[3,2,16,32,256]{4,3,2,1,0:T(8,128)} copy(f32[3,2,16,32,256]{4,3,2,1,0:T(8,128)S(1)} %bitcast.6) | data formatting | bytes 6291456
